TPU v7x, 32 devices: a whole 2x2x4 slice. The times are simulated.
32 devices in a mesh: seq: 8 (over z, y), batch: 4 (over x, core).
Axes of the slice: x: 2, y: 2, z: 4, core: 2. Of those that a mesh axis runs over, the one named last changes fastest.
Arguments:
- queries: bfloat16 [4, 4096, 16, 128], P('batch', 'seq'), may hold values from -5 to 5
- keys: bfloat16 [4, 4096, 16, 128], P('batch', 'seq'), may hold values from -5 to 5
- values: bfloat16 [4, 4096, 16, 128], P('batch', 'seq'), may hold values from -5 to 5
- keep_count: int32 [4, 16, 32], P('batch'), may hold values from 0 to 128
- query_map: bfloat16 [16, 128, 8], replicated, may hold values from -0.5 to 0.5
- key_map: bfloat16 [16, 128, 8], replicated, may hold values from -0.5 to 0.5
- cotangent: bfloat16 [4, 4096, 16, 128], P('batch', 'seq'), may hold values from -5 to 5
Outputs:
- attended: bfloat16 [4, 4096, 16, 128], P('batch', 'seq')
- grad_query_map: float32 [16, 128, 8], replicated
- grad_key_map: float32 [16, 128, 8], replicated
All inputs are finite; a program needn't handle non-finite values.
Results may differ from a plain program's by a relative error of at most 0.0035.
Values may be sent and summed in bfloat16 or wider, within the bound.
A program may use at most 128 MiB of HBM per device.

v0:
```python
import math

import jax
import jax.numpy as jnp
from jax import lax
from jax.sharding import PartitionSpec as P

TILE = 128
WINDOW = 256


HIGHEST = lax.Precision.HIGHEST
feature_shift = 1.5


def passed_along(value, axis, steps):
    count = lax.axis_size(axis)
    first, last = (max(0, -steps), min(count, count - steps))
    return lax.ppermute(value, axis, [(source, source + steps) for source in range(first, last)])


def prefix(shard, axis, combine, identity, reverse):
    peers, position = (lax.axis_size(axis), lax.axis_index(axis))
    everything = jax.tree.map(lambda part: lax.all_gather(part, axis), shard)
    start = jax.tree.map(
        lambda part, zero: jnp.broadcast_to(jnp.asarray(zero, part.dtype), part.shape),
        shard,
        identity,
    )

    def step(k, before):
        at = peers - 1 - k if reverse else k
        reached = at > position if reverse else at < position
        new = combine(before, jax.tree.map(lambda part: part[at], everything))
        return jax.tree.map(lambda a, b: jnp.where(reached, a, b), new, before)

    return lax.fori_loop(0, peers, step, start)


def add_pair(earlier, later):
    return (earlier[0] + later[0], earlier[1] + later[1])


def windowed(tiled, first, count, span):
    pieces = [
        lax.slice_in_dim(tiled, first + offset, first + offset + count, axis=0)
        for offset in range(span)
    ]
    return jnp.concatenate(pieces, 1)


def body(queries, keys, values, keep_count, query_map, key_map, cotangent):
    q_rows = queries[0]
    k_rows = keys[0]
    v_rows = values[0]
    cot_rows = cotangent[0].astype(jnp.float32)
    tokens, heads, width = q_rows.shape
    rank = query_map.shape[2]
    tiles_dev = tokens // TILE
    span = WINDOW // TILE
    scale = 1.0 / math.sqrt(width)
    index = lax.axis_index("seq")
    halo_rows = WINDOW - TILE
    prev_keys, prev_values = passed_along(
        (k_rows[tokens - halo_rows :], v_rows[tokens - halo_rows :]), "seq", 1
    )
    halo_tiles = halo_rows // TILE
    ext_tiles = halo_tiles + tiles_dev
    ext_rows = halo_rows + tokens
    ext_keys = jnp.concatenate([prev_keys, k_rows], 0)
    ext_values = jnp.concatenate([prev_values, v_rows], 0)
    counts = keep_count[0]
    padded_counts = jnp.concatenate([jnp.zeros((heads, tiles_dev), jnp.int32), counts], 1)
    count_start = index * tiles_dev + tiles_dev - halo_tiles
    ext_counts = lax.dynamic_slice_in_dim(padded_counts, count_start, ext_tiles, 1)
    local = jnp.arange(ext_rows, dtype=jnp.int32)
    key_pos = index * tokens - halo_rows + local
    valid = key_pos >= 0
    within = local % TILE
    kept = within[None, :] < jnp.repeat(ext_counts, TILE, axis=1)
    evicted = valid[None, :] & jnp.logical_not(kept)
    pre_q = (
        jnp.einsum("thd,hdr->thr", q_rows, query_map, preferred_element_type=jnp.float32)
        - feature_shift
    )
    pre_k = (
        jnp.einsum("thd,hdr->thr", ext_keys, key_map, preferred_element_type=jnp.float32)
        - feature_shift
    )
    feat_q = jax.nn.softplus(pre_q)
    feat_k = jax.nn.softplus(pre_k)
    valid_f = valid.astype(jnp.float32)[:, None, None]
    evict_f = evicted.T.astype(jnp.float32)[:, :, None]
    v_tiles = ext_values.astype(jnp.float32).reshape(ext_tiles, TILE, heads, width)

    def tile_state(feat):
        tiled = feat.reshape(ext_tiles, TILE, heads, rank)
        return (jnp.einsum("nthr,nthd->nhrd", tiled, v_tiles, precision=HIGHEST), jnp.sum(tiled, 1))

    all_state, all_norm = tile_state(feat_k * valid_f)
    ev_state, ev_norm = tile_state(feat_k * evict_f)
    q_tile = jnp.arange(tiles_dev, dtype=jnp.int32)[:, None] + halo_tiles
    k_tile = jnp.arange(ext_tiles, dtype=jnp.int32)[None, :]
    in_halo = (k_tile < halo_tiles).astype(jnp.float32)
    far_mix = (k_tile < q_tile - span + 1).astype(jnp.float32)
    near_mix = ((k_tile >= q_tile - span + 1) & (k_tile < q_tile)).astype(jnp.float32)
    far_coef = far_mix * (1.0 - in_halo) - near_mix * in_halo
    carried_state = jnp.sum(all_state[halo_tiles:], 0)
    carried_norm = jnp.sum(all_norm[halo_tiles:], 0)
    far_state, far_norm = prefix(
        (carried_state, carried_norm),
        "seq",
        add_pair,
        (jnp.zeros_like(carried_state), jnp.zeros_like(carried_norm)),
        False,
    )
    state = (
        far_state[None]
        + jnp.einsum("jn,nhrd->jhrd", far_coef, all_state, precision=HIGHEST)
        + jnp.einsum("jn,nhrd->jhrd", near_mix, ev_state, precision=HIGHEST)
    )
    norm = (
        far_norm[None]
        + jnp.einsum("jn,nhr->jhr", far_coef, all_norm, precision=HIGHEST)
        + jnp.einsum("jn,nhr->jhr", near_mix, ev_norm, precision=HIGHEST)
    )
    first_tile = halo_tiles - span + 1
    key_window = windowed(
        ext_keys.reshape(ext_tiles, TILE, heads, width), first_tile, tiles_dev, span
    )
    value_window = windowed(
        ext_values.reshape(ext_tiles, TILE, heads, width), first_tile, tiles_dev, span
    )
    allowed = (kept & valid[None, :]).T.reshape(ext_tiles, TILE, heads)
    allowed_window = windowed(allowed, first_tile, tiles_dev, span).transpose(0, 2, 1)
    slot = jnp.arange(span * TILE, dtype=jnp.int32)
    own_slot = slot >= (span - 1) * TILE
    causal = slot[None, :] - (span - 1) * TILE <= jnp.arange(TILE, dtype=jnp.int32)[:, None]
    live_pairs = jnp.where(
        own_slot[None, None, None, :], causal[None, None], allowed_window[:, :, None, :]
    )
    q_tiles = q_rows.reshape(tiles_dev, TILE, heads, width)
    scores = (
        jnp.einsum("nqhd,nkhd->nhqk", q_tiles, key_window, preferred_element_type=jnp.float32)
        * scale
    )
    row_max = jnp.max(jnp.where(live_pairs, scores, -jnp.inf), -1)
    weights = jnp.where(live_pairs, jnp.exp(scores - row_max[..., None]), 0.0)
    denom = jnp.sum(weights, -1).transpose(0, 2, 1).reshape(tokens, heads)
    numer = jnp.einsum(
        "nhqk,nkhd->nqhd",
        weights.astype(jnp.bfloat16),
        value_window,
        preferred_element_type=jnp.float32,
    ).reshape(tokens, heads, width)
    decay = jnp.exp(-row_max.transpose(0, 2, 1).reshape(tokens, heads))
    feat_qt = feat_q.reshape(tiles_dev, TILE, heads, rank)
    kernel_num = jnp.einsum("nthr,nhrd->nthd", feat_qt, state, precision=HIGHEST).reshape(
        tokens, heads, width
    )
    kernel_den = jnp.einsum("nthr,nhr->nth", feat_qt, norm, precision=HIGHEST).reshape(
        tokens, heads
    )
    total = denom + decay * kernel_den
    out = (numer + decay[..., None] * kernel_num) / total[..., None]
    delta = cot_rows / total[..., None]
    ratio_grad = -jnp.sum(delta * out, -1)
    grad_num = (decay[..., None] * delta).reshape(tiles_dev, TILE, heads, width)
    grad_den = (decay * ratio_grad).reshape(tiles_dev, TILE, heads)
    grad_fq = (
        jnp.einsum("nthd,nhrd->nthr", grad_num, state, precision=HIGHEST)
        + grad_den[..., None] * norm[:, None]
    )
    d_state = jnp.einsum("nthr,nthd->nhrd", feat_qt, grad_num, precision=HIGHEST)
    d_norm = jnp.einsum("nthr,nth->nhr", feat_qt, grad_den, precision=HIGHEST)
    own_state = jnp.sum(d_state, 0)
    own_norm = jnp.sum(d_norm, 0)
    after_state, after_norm = prefix(
        (own_state, own_norm),
        "seq",
        add_pair,
        (jnp.zeros_like(own_state), jnp.zeros_like(own_norm)),
        True,
    )
    own_tiles = (jnp.arange(ext_tiles, dtype=jnp.int32) >= halo_tiles).astype(jnp.float32)
    d_all = (
        jnp.einsum("jn,jhrd->nhrd", far_coef, d_state, precision=HIGHEST)
        + own_tiles[:, None, None, None] * after_state[None]
    )
    d_alln = (
        jnp.einsum("jn,jhr->nhr", far_coef, d_norm, precision=HIGHEST)
        + own_tiles[:, None, None] * after_norm[None]
    )
    d_ev = jnp.einsum("jn,jhrd->nhrd", near_mix, d_state, precision=HIGHEST)
    d_evn = jnp.einsum("jn,jhr->nhr", near_mix, d_norm, precision=HIGHEST)
    grad_all = jnp.einsum("nhrd,nthd->nthr", d_all, v_tiles, precision=HIGHEST) + d_alln[:, None]
    grad_ev = jnp.einsum("nhrd,nthd->nthr", d_ev, v_tiles, precision=HIGHEST) + d_evn[:, None]
    grad_fk = valid_f * grad_all.reshape(ext_rows, heads, rank) + evict_f * grad_ev.reshape(
        ext_rows, heads, rank
    )
    grad_pre_k = grad_fk * jax.nn.sigmoid(pre_k)
    grad_pre_q = grad_fq.reshape(tokens, heads, rank) * jax.nn.sigmoid(pre_q)
    grad_q = jnp.einsum("thd,thr->hdr", q_rows.astype(jnp.float32), grad_pre_q, precision=HIGHEST)
    grad_k = jnp.einsum("thd,thr->hdr", ext_keys.astype(jnp.float32), grad_pre_k, precision=HIGHEST)
    grad_q, grad_k = lax.psum((grad_q, grad_k), ("seq", "batch"))
    return (out.astype(jnp.bfloat16)[None], grad_q, grad_k)


def solution(mesh):
    placed = (
        P("batch", "seq", None, None),
        P("batch", "seq", None, None),
        P("batch", "seq", None, None),
        P("batch", None, None),
        P(),
        P(),
        P("batch", "seq", None, None),
    )
    return jax.shard_map(
        body,
        mesh=mesh,
        in_specs=placed,
        out_specs=(P("batch", "seq", None, None), P(), P()),
        check_vma=False,
    )
```

profile of v0, /device:TPU:0, one launch (start us, length us, event | category | flops | bytes accessed | tf_op | source)
XLA Modules:
  0.0 420.2 jit_solution(9056168187303462686)
XLA Ops:
  11.7 5.7 %collective-permute-start.1 = (bf16[128,16,128]{2,0,1:T(8,128)(2,1)}, bf16[128,16,128]{2,0,1:T(8,128)(2,1)}, u32[]{:S(2)}, u32[]{:S(2)}) collective-permute-start(bf16[128,16,128]{2,0,1:T(8,128)(2,1)} %slice_bitcast_fusion), channel_id=1, source_target_pairs={{0,4},{4,8},{8,12},{12,16},{16,20},{20,24},{24,28},{1,5},{5,9},{9,... | collective-permute-start | bytes 1572872 | tf_op jit(solution)/shard_map/ppermute | solution.py:19
  19.3 2.7 collective-permute-start
  26.0 3.5 copy.177
  45.3 35.2 %all-gather = f32[128,8,128]{2,1,0:T(8,128)} all-gather(f32[16,8,128]{2,1,0:T(8,128)S(1)} %slice_reduce_fusion), channel_id=2, replica_groups=mesh['seq'=8,'batch'=4] {'seq'}, dimensions={0}, use_global_device_ids=true | all-gather | bytes 589824 | tf_op jit(solution)/shard_map/all_gather | solution.py:24
  80.6 30.6 %all-gather.4 = f32[8,16,8]{1,2,0:T(8,128)S(1)} all-gather(f32[1,16,8]{1,2,0:T(8,128)S(1)} %bitcast.246), channel_id=3, replica_groups=mesh['seq'=8,'batch'=4] {'seq'}, dimensions={0}, use_global_device_ids=true | all-gather | bytes 4608 | tf_op jit(solution)/shard_map/all_gather | solution.py:24
  111.2 7.7 %while.34 = (s32[]{:T(128)}, f32[16,8,128]{2,1,0:T(8,128)S(1)}, f32[16,8]{0,1:T(8,128)S(1)}, s32[]{:T(128)}, f32[8,16,8,128]{3,2,1,0:T(8,128)}, /*index=5*/f32[8,16,8]{1,2,0:T(8,128)S(1)}, s32[]{:T(128)}, s32[]{:T(128)}) while((s32[]{:T(128)}, f32[16,8,128]{2,1,0:T(8,128)S(1)}, f32[16,8]{0,1:T(8,128)S(1)}, s32[]{:T(128)}, ...), condition=%wide.region_5.6_spmd.clone, body=%wide.region_4.5_spmd.clone.sunk | while | flops 49540 | bytes 198259 | solution.py:37
  118.9 3.9 fusion.42
  124.9 6.7 %convolution_bitcast_fusion = f32[4,128,16,128]{3,1,2,0:T(8,128)S(1)} fusion(f32[4,16,8,128]{3,0,2,1:T(4,128)S(1)} %fusion.66, f32[512,16,8]{0,2,1:T(8,128)S(1)} %copy-done.13), kind=kOutput, calls=%fused_computation.42 | convolution fusion | flops 101056512 | bytes 4718592 | tf_op jit(solution)/shard_map/nthr,nhrd->nthd/dot_general | solution.py:158
  131.6 4.5 %copy.193 = f32[4,128,16,128]{3,2,1,0:T(8,128)} copy(f32[4,128,16,128]{3,1,2,0:T(8,128)S(1)} %convolution_bitcast_fusion) | data formatting | bytes 8388608 | tf_op jit(solution)/shard_map/nthr,nhrd->nthd/transpose | solution.py:158
  139.9 2.9 fusion
  143.5 4.1 fusion.2
  152.3 6.3 %fusion.27 = f32[4,128,16,128]{3,1,2,0:T(8,128)S(1)} fusion(f32[4,16,256,128]{3,2,1,0:T(8,128)S(1)} %copy-done.10, f32[4,16,128]{2,1,0:T(8,128)S(1)} %get-tuple-element.356, pred[4,16,256]{2,1,0:T(8,128)(4,1)S(1)} %copy-done.26, pred[128,256]{0,1:T(8,128)(4,1)S(1)} %copy-done.21, pred[256]{0:T(512)(128)(4,1)S(1)} %copy-done.42, ...), kind=kOutput, calls=%fused_computation.41 | convolution fusion | flops 555745280 | bytes 16859392 | tf_op jit(solution)/shard_map/nhqk,nkhd->nqhd/dot_general | solution.py:150
  158.6 4.4 %copy.180 = f32[4,128,16,128]{3,2,1,0:T(8,128)} copy(f32[4,128,16,128]{3,1,2,0:T(8,128)S(1)} %fusion.27) | data formatting | bytes 8388608 | tf_op jit(solution)/shard_map/nhqk,nkhd->nqhd/transpose | solution.py:150
  163.1 6.9 %fusion.14 = f32[512,16,128]{2,1,0:T(8,128)S(1)} fusion(f32[4,128,16,128]{3,2,1,0:T(8,128)} %copy.193, f32[4,128,16,128]{3,2,1,0:T(8,128)} %copy.180, f32[512,16]{1,0:T(8,128)S(1)} %copy.182, f32[512,16]{1,0:T(8,128)S(1)} %copy.198), kind=kLoop, calls=%fused_computation.21 | loop fusion | flops 3145728 | bytes 12648448 | tf_op jit(solution)/shard_map/div | solution.py:165
  170.0 14.1 %fusion.23 = f32[512,16]{1,0:T(8,128)S(1)} fusion(f32[512,16,128]{2,1,0:T(8,128)S(1)} %fusion.14, f32[512,16]{1,0:T(8,128)S(1)} %copy.198, bf16[1,512,16,128]{3,2,1,0:T(8,128)(2,1)S(1)} %copy-done.8), kind=kLoop, calls=%fused_computation.33 | loop fusion | flops 4186112 | bytes 6356992 | tf_op jit(solution)/shard_map/reduce_sum | solution.py:167
  186.7 7.5 %fusion.174 = (f32[16,8,128]{2,1,0:T(8,128)S(1)}, f32[4,16,8,128]{3,2,1,0:T(8,128)}) fusion(f32[4,128,16,128]{3,2,1,0:T(8,128)} %convert.3, f32[4,128,16]{1,2,0:T(8,128)S(1)} %get-tuple-element.351, f32[4,128,16]{1,2,0:T(8,128)S(1)} %copy-done.28, f32[512,16,8]{0,2,1:T(8,128)S(1)} %copy-done.14), kind=kOutput, calls=%fused_computation.200 | convolution fusion | flops 103202816 | bytes 4849664 | tf_op jit(solution)/shard_map/nthr,nthd->nhrd/dot_general | solution.py:174
  194.2 31.2 %all-gather.2 = f32[128,8,128]{2,1,0:T(8,128)S(1)} all-gather(f32[16,8,128]{2,1,0:T(8,128)S(1)} %get-tuple-element.358), channel_id=4, replica_groups=mesh['seq'=8,'batch'=4] {'seq'}, dimensions={0}, use_global_device_ids=true | all-gather | bytes 589824 | tf_op jit(solution)/shard_map/all_gather | solution.py:24
  225.4 30.6 %all-gather.5 = f32[8,16,8]{1,2,0:T(8,128)S(1)} all-gather(f32[1,16,8]{1,2,0:T(8,128)S(1)} %bitcast.245), channel_id=5, replica_groups=mesh['seq'=8,'batch'=4] {'seq'}, dimensions={0}, use_global_device_ids=true | all-gather | bytes 4608 | tf_op jit(solution)/shard_map/all_gather | solution.py:24
  262.2 9.5 %fusion.76 = f32[4,128,16,8]{1,3,2,0:T(8,128)S(1)} fusion(f32[4,128,16,128]{3,2,1,0:T(8,128)} %convert.3, f32[4,128,16]{1,2,0:T(8,128)} %copy-done.31, f32[4,128,16]{1,2,0:T(8,128)} %get-tuple-element.352, f32[4,16,8,128]{3,0,2,1:T(4,128)} %copy-done.15, f32[4,16,8]{2,1,0:T(8,128)} %copy.207, f32[4,128,16]{1,2,0:T(8,128)} %copy-done.30), kind=kOutput, calls=%fused_computation.74 | convolution fusion | flops 102891520 | bytes 4818944 | tf_op jit(solution)/shard_map/nthd,nhrd->nthr/dot_general | solution.py:171
  273.7 4.1 fusion.51
  277.9 4.1 fusion.57
  282.1 3.1 fusion.47
  285.1 7.2 %fusion.18 = bf16[1,512,16,128]{3,2,1,0:T(8,128)(2,1)} fusion(f32[512,16]{1,0:T(8,128)S(1)} %copy.198, f32[512,16]{1,0:T(8,128)S(1)} %copy.182, f32[1,512,16,128]{3,2,1,0:T(8,128)} %bitcast.221, f32[1,512,16,128]{3,2,1,0:T(8,128)} %bitcast.222), kind=kLoop, calls=%fused_computation.27 | loop fusion | flops 4194304 | bytes 10551296 | tf_op jit(solution)/shard_map/convert_element_type | solution.py:206
  292.4 117.7 %all-reduce.4.cloned.1.call-done = (f32[16,128,8]{1,2,0:T(8,128)}, f32[16,128,8]{1,2,0:T(8,128)}) async-done(((f32[16,128,8]{1,2,0:T(8,128)}, f32[16,128,8]{1,2,0:T(8,128)}), (f32[16,128,8]{1,2,0:T(8,128)}, f32[16,128,8]{1,2,0:T(8,128)})) %all-reduce.4.cloned.1.call-update) | async-done | bytes 131088 | tf_op jit(solution)/shard_map/psum | solution.py:205
  (194 shorter events, 58.0 us)
Async XLA Ops:
  7.2 26.6 %copy-start = (bf16[1,512,16,128]{3,2,1,0:T(8,128)(2,1)S(1)}, bf16[1,512,16,128]{3,2,1,0:T(8,128)(2,1)}, u32[]{:S(2)}) copy-start(bf16[1,512,16,128]{3,2,1,0:T(8,128)(2,1)} %param.11) | copy-start | bytes 6291460
  7.2 16.6 %copy-start.37 = (s32[1,16,32]{2,1,0:T(8,128)S(1)}, s32[1,16,32]{2,1,0:T(8,128)}, u32[]{:S(2)}) copy-start(s32[1,16,32]{2,1,0:T(8,128)} %param.14) | copy-start | bytes 6148
  7.2 402.9 %all-reduce.4.cloned.1.call-start = ((), (), s32[]{:S(2)}) async-start(), calls=%async_computation | async-start | bytes 262144 | tf_op jit(solution)/shard_map/psum | solution.py:205
  11.7 23.6 %collective-permute-start.1 = (bf16[128,16,128]{2,0,1:T(8,128)(2,1)}, bf16[128,16,128]{2,0,1:T(8,128)(2,1)}, u32[]{:S(2)}, u32[]{:S(2)}) collective-permute-start(bf16[128,16,128]{2,0,1:T(8,128)(2,1)} %slice_bitcast_fusion), channel_id=1, source_target_pairs={{0,4},{4,8},{8,12},{12,16},{16,20},{20,24},{24,28},{1,5},{5,9},{9,... | collective-permute-start | bytes 1572872 | tf_op jit(solution)/shard_map/ppermute | solution.py:19
  19.3 20.4 %collective-permute-start = (bf16[128,16,128]{2,1,0:T(8,128)(2,1)}, bf16[128,16,128]{2,1,0:T(8,128)(2,1)S(1)}, u32[]{:S(2)}, u32[]{:S(2)}) collective-permute-start(bf16[128,16,128]{2,1,0:T(8,128)(2,1)} %slice_bitcast_fusion.1), channel_id=1, source_target_pairs={{0,4},{4,8},{8,12},{12,16},{16,20},{20,24},{24,28},{1,5},{5,9},{9,... | collective-permute-start | bytes 1572872 | tf_op jit(solution)/shard_map/ppermute | solution.py:19
  22.0 15.3 %copy-start.32 = (f32[640]{0:T(1024)}, f32[640]{0:T(1024)S(1)}, u32[]{:S(2)}) copy-start(f32[640]{0:T(1024)S(1)} %fusion.149) | copy-start | bytes 7684
  22.0 114.2 %copy-start.34 = (s32[4]{0:T(128)}, s32[4]{0:T(128)S(1)}, u32[]{:S(2)}) copy-start(s32[4]{0:T(128)S(1)} %iota_add_fusion.1) | copy-start | bytes 52
  111.2 12.2 %copy-start.38 = (f32[5]{0:T(128)S(1)}, f32[5]{0:T(128)}, u32[]{:S(2)}) copy-start(f32[5]{0:T(128)} %broadcast_subtract_fusion) | copy-start | bytes 64
  111.2 12.2 %copy-start.40 = (f32[5]{0:T(128)S(1)}, f32[5]{0:T(128)}, u32[]{:S(2)}) copy-start(f32[5]{0:T(128)} %compare_convert_fusion.1) | copy-start | bytes 64
  118.9 6.0 %copy-start.13 = (f32[512,16,8]{0,2,1:T(8,128)S(1)}, f32[512,16,8]{0,2,1:T(8,128)}, u32[]{:S(2)}) copy-start(f32[512,16,8]{0,2,1:T(8,128)} %fusion.73) | copy-start | bytes 786436
  131.6 5.8 %copy-start.14 = (f32[512,16,8]{0,2,1:T(8,128)S(1)}, f32[512,16,8]{0,2,1:T(8,128)}, u32[]{:S(2)}) copy-start(f32[512,16,8]{0,2,1:T(8,128)} %fusion.73) | copy-start | bytes 786436
  138.2 10.1 %copy-start.23 = (f32[4,16,1,128]{3,2,1,0:T(1,128)}, f32[4,16,1,128]{3,2,1,0:T(1,128)S(1)}, u32[]{:S(2)}) copy-start(f32[4,16,1,128]{3,2,1,0:T(1,128)S(1)} %fusion.112) | copy-start | bytes 98308
  142.8 4.8 %copy-start.9 = (f32[4,16,256,128]{3,2,1,0:T(8,128)}, f32[4,16,256,128]{3,2,1,0:T(8,128)S(1)}, u32[]{:S(2)}) copy-start(f32[4,16,256,128]{3,2,1,0:T(8,128)S(1)} %get-tuple-element.357) | copy-start | bytes 25165828
  163.1 6.9 %copy-start.8 = (bf16[1,512,16,128]{3,2,1,0:T(8,128)(2,1)S(1)}, bf16[1,512,16,128]{3,2,1,0:T(8,128)(2,1)}, u32[]{:S(2)}) copy-start(bf16[1,512,16,128]{3,2,1,0:T(8,128)(2,1)} %param.17) | copy-start | bytes 6291460
  170.0 14.2 %copy-start.24 = (f32[4,16,1,128]{3,2,1,0:T(1,128)S(1)}, f32[4,16,1,128]{3,2,1,0:T(1,128)}, u32[]{:S(2)}) copy-start(f32[4,16,1,128]{3,2,1,0:T(1,128)} %copy-done.23) | copy-start | bytes 98308
  170.0 15.0 %copy-start.35 = (s32[4]{0:T(128)S(1)}, s32[4]{0:T(128)}, u32[]{:S(2)}) copy-start(s32[4]{0:T(128)} %copy-done.34) | copy-start | bytes 52
  170.0 16.6 %copy-start.28 = (f32[4,128,16]{1,2,0:T(8,128)S(1)}, f32[4,128,16]{1,2,0:T(8,128)}, u32[]{:S(2)}) copy-start(f32[4,128,16]{1,2,0:T(8,128)} %get-tuple-element.352) | copy-start | bytes 98308
  184.3 9.9 %copy-start.30 = (f32[4,128,16]{1,2,0:T(8,128)}, f32[4,128,16]{1,2,0:T(8,128)S(1)}, u32[]{:S(2)}) copy-start(f32[4,128,16]{1,2,0:T(8,128)S(1)} %get-tuple-element.350) | copy-start | bytes 98308
  184.3 9.9 %copy-start.31 = (f32[4,128,16]{1,2,0:T(8,128)}, f32[4,128,16]{1,2,0:T(8,128)S(1)}, u32[]{:S(2)}) copy-start(f32[4,128,16]{1,2,0:T(8,128)S(1)} %get-tuple-element.351) | copy-start | bytes 98308
  186.6 69.3 %copy-start.25 = (f32[16,8]{0,1:T(8,128)S(1)}, f32[16,8]{0,1:T(8,128)}, u32[]{:S(2)}) copy-start(f32[16,8]{0,1:T(8,128)} %custom-call.3) | copy-start | bytes 1540
  186.6 70.1 %copy-start.36 = (s32[4]{0:T(128)S(1)}, s32[4]{0:T(128)}, u32[]{:S(2)}) copy-start(s32[4]{0:T(128)} %copy-done.34) | copy-start | bytes 52
  186.6 70.1 %copy-start.39 = (f32[5]{0:T(128)S(1)}, f32[5]{0:T(128)}, u32[]{:S(2)}) copy-start(f32[5]{0:T(128)} %broadcast_subtract_fusion) | copy-start | bytes 64
  186.6 70.1 %copy-start.41 = (f32[5]{0:T(128)S(1)}, f32[5]{0:T(128)}, u32[]{:S(2)}) copy-start(f32[5]{0:T(128)} %compare_convert_fusion.1) | copy-start | bytes 64
  186.6 70.1 %copy-start.43 = (f32[5]{0:T(128)S(1)}, f32[5]{0:T(128)}, u32[]{:S(2)}) copy-start(f32[5]{0:T(128)} %compare_convert_fusion) | copy-start | bytes 64
  (24 other events, 70.9 us)
Sparse Core Ops, SparseCore 0:
  285.3 124.7 all-reduce.3
where the time goes:
time: 427 us; the launch traced here: 420 us
  blocking collectives  128 us (30%)
  waiting for transfers between devices  118 us (28%)
  matrix products  64.9 us (15%)
  other arithmetic  52 us (12%)
  local copies, waits for them, and re-layouts  33.3 us (8%)
  between operations  15.1 us (4%)
  starting transfers between devices  8.39 us (2%)
    all_gather x4, blocking collectives, prefix(): everything = jax.tree.map(lambda part: lax.all_gather(part, axis), shard)  128 us
    psum x1, waiting for transfers between devices, body(): grad_q, grad_k = lax.psum((grad_q, grad_k), ('seq', 'batch'))  118 us
    reduce_sum x1, other arithmetic, body(): ratio_grad = -jnp.sum(delta * out, -1)  14.1 us
    unnamed x93, local copies, waits for them, and re-layouts  11.3 us
    dot_general x1, matrix products, body(): jnp.einsum('nthd,nhrd->nthr', grad_num, state, precision=HIGHEST)  9.54 us
  transfers between devices with their start and end apart: 3, of which 1 were waited for; matrix products, arithmetic and copies ran while one was open for 6% of the time, Pallas kernels for 0%

commit v1 on v0

v1 whole, which is shorter than its diff:
```python
import functools
import math

import jax
import jax.numpy as jnp
from jax import lax
from jax.experimental import pallas as pl
from jax.experimental.pallas import tpu as pltpu
from jax.sharding import PartitionSpec as P

TILE = 128
SHIFT = 1.5
LOG2E = 1.0 / math.log(2.0)
MASKED = -1e30
F32 = jnp.float32
BF16 = jnp.bfloat16
VMEM_LIMIT = 56 * 1024 * 1024


def dot_nt(a, b):
    return lax.dot_general(a, b, (((1,), (1,)), ((), ())), preferred_element_type=F32)


def dot_nn(a, b):
    return lax.dot_general(a, b, (((1,), (0,)), ((), ())), preferred_element_type=F32)


def dot_tn(a, b):
    return lax.dot_general(a, b, (((0,), (0,)), ((), ())), preferred_element_type=F32)


def by_head(x):
    return jnp.swapaxes(x, 0, 1)


def softplus(x):
    return jnp.maximum(x, 0.0) + jnp.log1p(jnp.exp(-jnp.abs(x)))


def sigmoid(x):
    return 1.0 / (1.0 + jnp.exp(-x))


def halves(x):
    top = x.astype(BF16)
    return top, (x - top.astype(F32)).astype(BF16)


def split_dot(dot, x, y):
    rows = x.shape[0]
    both = dot(jnp.concatenate(halves(x), 0), y)
    return both[:rows] + both[rows:]


def with_ones(v):
    return jnp.concatenate([v, jnp.ones(v.shape, v.dtype)], 1)


def state_kernel(k_ref, v_ref, wk_ref, kh_ref, vh_ref, total_ref, acc_ref):
    step = pl.program_id(0)
    heads = wk_ref.shape[0]
    kh_ref[...] = by_head(k_ref[...])
    vh_ref[...] = by_head(v_ref[...])

    @pl.when(step == 0)
    def _():
        acc_ref[...] = jnp.zeros_like(acc_ref)

    def one_head(h, carry):
        feat = softplus(dot_nt(wk_ref[h], kh_ref[h]) - SHIFT)
        acc_ref[h] += split_dot(dot_nn, feat, with_ones(vh_ref[h]))
        return carry

    lax.fori_loop(0, heads, one_head, 0, unroll=4)

    @pl.when(step == pl.num_programs(0) - 1)
    def _():
        total_ref[...] = acc_ref[...]


def local_states(k_rows, v_rows, wk):
    tokens, heads, width = k_rows.shape
    rank = wk.shape[1]
    row_spec = pl.BlockSpec((TILE, heads, width), lambda n: (n, 0, 0))
    head_spec = pl.BlockSpec((heads, TILE, width), lambda n: (0, n, 0))
    return pl.pallas_call(
        state_kernel,
        name="local_states",
        grid=(tokens // TILE,),
        in_specs=[row_spec, row_spec, pl.BlockSpec(wk.shape, lambda n: (0, 0, 0))],
        out_specs=[head_spec, head_spec, pl.BlockSpec((heads, rank, 2 * width), lambda n: (0, 0, 0))],
        out_shape=[
            jax.ShapeDtypeStruct((heads, tokens, width), BF16),
            jax.ShapeDtypeStruct((heads, tokens, width), BF16),
            jax.ShapeDtypeStruct((heads, rank, 2 * width), F32),
        ],
        scratch_shapes=[pltpu.VMEM((heads, rank, 2 * width), F32)],
        compiler_params=pltpu.CompilerParams(vmem_limit_bytes=VMEM_LIMIT),
        cost_estimate=pl.CostEstimate(flops=10**9, bytes_accessed=8 * 2**20, transcendentals=10**6),
    )(k_rows, v_rows, wk)


def main_kernel(
    first, halo, counts_ref, where_ref, q_ref, k_ref, v_ref, kp_ref, vp_ref, c_ref, wq_ref, wk_ref,
    states_ref, out_ref, ds_ref, gq_ref, gk_ref, qh, ch, oh, kph, vph, run,
):
    step = pl.program_id(0)
    heads = wq_ref.shape[0]
    peers = states_ref.shape[0]
    width = q_ref.shape[2]
    me = where_ref[0]
    tiles_dev = where_ref[1]
    factor = LOG2E / math.sqrt(width)
    qh[...] = by_head(q_ref[...])
    ch[...] = by_head(c_ref[...])
    if halo:
        kph[...] = by_head(kp_ref[...])
        vph[...] = by_head(vp_ref[...])
    prev_k = kph if halo else kp_ref
    prev_v = vph if halo else vp_ref

    @pl.when(step == 0)
    def _():
        gq_ref[...] = jnp.zeros_like(gq_ref)
        gk_ref[...] = jnp.zeros_like(gk_ref)
        before = jnp.zeros(run.shape, F32)
        for peer in range(peers):
            before += jnp.where(peer < me, states_ref[peer].astype(F32), 0.0)
        run[...] = before

    tile = me * tiles_dev + first + step
    lane = lax.broadcasted_iota(jnp.int32, (1, TILE), 1)
    row = lax.broadcasted_iota(jnp.int32, (TILE, TILE), 0)
    col = lax.broadcasted_iota(jnp.int32, (TILE, TILE), 1)
    causal = col <= row

    def one_head(h, carry):
        q, c = qh[h], ch[h]
        k, v = k_ref[h], v_ref[h]
        kp, vp = prev_k[h], prev_v[h]
        count = jnp.where(tile > 0, counts_ref[h, jnp.maximum(tile - 1, 0)], 0)
        kept = lane < count
        kept_f = kept.astype(F32)
        pre_p = dot_nt(wk_ref[h], kp) - SHIFT
        feat_p = softplus(pre_p)
        vp_ext = with_ones(vp)
        rank = feat_p.shape[0]
        both = split_dot(dot_nn, jnp.concatenate([feat_p, feat_p * kept_f], 0), vp_ext)
        if halo:
            state = run[h] - both[rank:]
        else:
            total = run[h] + both[:rank]
            run[h] = total
            state = total - both[rank:]
        own = jnp.where(causal, dot_nt(q, k), MASKED)
        old = jnp.where(kept, dot_nt(q, kp), MASKED)
        top = jnp.max(jnp.maximum(own, old), 1, keepdims=True) * factor
        p_own = jnp.exp2(own * factor - top).astype(BF16)
        p_old = jnp.exp2(old * factor - top).astype(BF16)
        numer = dot_nn(p_own, with_ones(v)) + dot_nn(p_old, vp_ext)
        decay = jnp.exp2(-top)
        pre_q = dot_nt(wq_ref[h], q) - SHIFT
        feat_q = softplus(pre_q)
        fq_top, fq_low = halves(feat_q)
        st_top, st_low = halves(state)
        kernel = dot_tn(jnp.concatenate([fq_top, fq_low, fq_top], 0), jnp.concatenate([st_top, st_top, st_low], 0))
        full = numer + decay * kernel
        inv = 1.0 / full[:, width:]
        out = full[:, :width] * inv
        oh[h] = out.astype(BF16)
        gn = decay * (c.astype(F32) * inv)
        g_ext = jnp.concatenate([gn, gn * out], 1).astype(BF16)
        signed = jnp.concatenate([state[:, :width], -state[:, width:]], 1)
        dpre_q = split_dot(dot_nt, signed, g_ext) * sigmoid(pre_q)
        gq_ref[h] += split_dot(dot_nn, dpre_q, q)
        ds = split_dot(dot_nn, feat_q, g_ext)
        ds_ref[0, h] = ds
        dn = -jnp.sum(ds[:, width:], 1, keepdims=True)
        dfk = split_dot(dot_nt, ds[:, :width], vp) + dn
        dpre_k = -kept_f * dfk * sigmoid(pre_p)
        gk_ref[h] += split_dot(dot_nn, dpre_k, kp)
        return carry

    lax.fori_loop(0, heads, one_head, 0, unroll=4)
    out_ref[...] = by_head(oh[...])


def attend(first, steps, halo, counts, where, q_rows, kh, vh, kp, vp, cot, wq, wk, states):
    tokens, heads, width = q_rows.shape
    rank = wq.shape[1]
    row_spec = pl.BlockSpec((TILE, heads, width), lambda n: (n + first, 0, 0))
    head_spec = pl.BlockSpec((heads, TILE, width), lambda n: (0, n + first, 0))
    if halo:
        prev_spec = pl.BlockSpec((TILE, heads, width), lambda n: (0, 0, 0))
    else:
        prev_spec = pl.BlockSpec((heads, TILE, width), lambda n: (0, n + first - 1, 0))
    whole = pl.BlockSpec((heads, rank, width), lambda n: (0, 0, 0))
    smem = pl.BlockSpec(memory_space=pltpu.SMEM)
    tile_scratch = pltpu.VMEM((heads, TILE, width), BF16)
    return pl.pallas_call(
        functools.partial(main_kernel, first, halo),
        name="attend_first" if halo else "attend_rest",
        grid=(steps,),
        in_specs=[
            smem, smem, row_spec, head_spec, head_spec, prev_spec, prev_spec, row_spec, whole, whole,
            pl.BlockSpec(states.shape, lambda n: (0, 0, 0, 0)),
        ],
        out_specs=[
            pl.BlockSpec((TILE, heads, width), lambda n: (n, 0, 0)),
            pl.BlockSpec((1, heads, rank, 2 * width), lambda n: (n, 0, 0, 0)),
            whole,
            whole,
        ],
        out_shape=[
            jax.ShapeDtypeStruct((steps * TILE, heads, width), BF16),
            jax.ShapeDtypeStruct((steps, heads, rank, 2 * width), F32),
            jax.ShapeDtypeStruct((heads, rank, width), F32),
            jax.ShapeDtypeStruct((heads, rank, width), F32),
        ],
        scratch_shapes=[tile_scratch] * 5 + [pltpu.VMEM((heads, rank, 2 * width), F32)],
        compiler_params=pltpu.CompilerParams(vmem_limit_bytes=VMEM_LIMIT),
        cost_estimate=pl.CostEstimate(flops=10**9 * steps, bytes_accessed=steps * 4 * 2**20, transcendentals=10**6),
    )(counts, where, q_rows, kh, vh, kp, vp, cot, wq, wk, states)


def key_kernel(where_ref, kh_ref, vh_ref, wk_ref, ds0_ref, ds1_ref, after_ref, gk_ref):
    group, tokens, width = kh_ref.shape
    tiles = tokens // TILE
    me = where_ref[0]
    for h in range(group):
        later = jnp.zeros(ds0_ref.shape[2:], F32)
        for peer in range(after_ref.shape[0]):
            later += jnp.where(peer > me, after_ref[peer, h].astype(F32), 0.0)
        pre = dot_nt(wk_ref[h], kh_ref[h]) - SHIFT
        pieces = [None] * tiles
        for n in reversed(range(tiles)):
            dn = -jnp.sum(later[:, width:], 1, keepdims=True)
            pieces[n] = split_dot(dot_nt, later[:, :width], vh_ref[h, n * TILE : (n + 1) * TILE]) + dn
            if n:
                later += ds1_ref[n - 1, h]
        grad = jnp.concatenate(pieces, 1) * sigmoid(pre)
        gk_ref[h] = split_dot(dot_nn, grad, kh_ref[h])


def key_grads(where, kh, vh, wk, ds0, ds1, after):
    heads, tokens, width = kh.shape
    rank = wk.shape[1]
    group = 4
    head_spec = pl.BlockSpec((group, tokens, width), lambda n: (n, 0, 0))
    whole = pl.BlockSpec((group, rank, width), lambda n: (n, 0, 0))

    def four(a):
        return pl.BlockSpec((a.shape[0], group) + a.shape[2:], lambda n: (0, n, 0, 0))

    return pl.pallas_call(
        key_kernel,
        name="key_grads",
        grid=(heads // group,),
        in_specs=[
            pl.BlockSpec(memory_space=pltpu.SMEM), head_spec, head_spec, whole, four(ds0), four(ds1), four(after),
        ],
        out_specs=whole,
        out_shape=jax.ShapeDtypeStruct((heads, rank, width), F32),
        compiler_params=pltpu.CompilerParams(vmem_limit_bytes=VMEM_LIMIT),
        cost_estimate=pl.CostEstimate(flops=10**9, bytes_accessed=8 * 2**20, transcendentals=10**6),
    )(where, kh, vh, wk, ds0, ds1, after)


def body(queries, keys, values, keep_count, query_map, key_map, cotangent):
    q_rows, k_rows, v_rows, cot = queries[0], keys[0], values[0], cotangent[0]
    counts = keep_count[0]
    tokens = q_rows.shape[0]
    tiles = tokens // TILE
    peers = lax.axis_size("seq")
    me = lax.axis_index("seq")
    where = jnp.stack([me, jnp.int32(tiles)]).astype(jnp.int32)
    ring = [(a, a + 1) for a in range(peers - 1)]
    kp, vp = lax.ppermute((k_rows[tokens - TILE :], v_rows[tokens - TILE :]), "seq", ring)
    wq = jnp.swapaxes(query_map, 1, 2)
    wk = jnp.swapaxes(key_map, 1, 2)
    kh, vh, total = local_states(k_rows, v_rows, wk)
    states = lax.all_gather(total, "seq")
    rest = attend(1, tiles - 1, False, counts, where, q_rows, kh, vh, kh, vh, cot, wq, wk, states)
    head = attend(0, 1, True, counts, where, q_rows, kh, vh, kp, vp, cot, wq, wk, states)
    own = head[1][0] + jnp.sum(rest[1], 0)
    after = lax.all_gather(own, "seq")
    gk = key_grads(where, kh, vh, wk, head[1], rest[1], after)
    grads = jnp.stack([head[2] + rest[2], head[3] + rest[3] + gk])
    grads = lax.psum(grads, ("seq", "batch"))
    grads = jnp.swapaxes(grads, 2, 3)
    out = jnp.concatenate([head[0], rest[0]], 0)
    return out[None], grads[0], grads[1]


def solution(mesh):
    placed = (
        P("batch", "seq", None, None),
        P("batch", "seq", None, None),
        P("batch", "seq", None, None),
        P("batch", None, None),
        P(),
        P(),
        P("batch", "seq", None, None),
    )
    return jax.shard_map(
        body,
        mesh=mesh,
        in_specs=placed,
        out_specs=(P("batch", "seq", None, None), P(), P()),
        check_vma=False,
    )
```

time: 427 us -> 320 us (0.75); the launches traced: 420 us -> 319 us
  blocking collectives: 128 us -> 0 us
  Pallas kernels: 0 us -> 89.5 us
  waiting for transfers between devices: 118 us -> 195 us
  matrix products: 64.9 us -> 0 us
  other arithmetic: 52 us -> 7.17 us
  local copies, waits for them, and re-layouts: 33.3 us -> 5.34 us
    all_gather x4 -> x0, blocking collectives: 128 us -> none  [prefix(): everything = jax.tree.map(lambda part: lax.all_gather(part, axis), shard)]
    pallas_call x0 -> x4, Pallas kernels: none -> 89.5 us  [the longest x2 66.7 us: attend(): pl.pallas_call(functools.partial(main_kernel, first, halo), name='attend_...]
    all_gather x0 -> x2, waiting for transfers between devices: none -> 73.3 us  [the longest x1 38.3 us: body(): after = lax.all_gather(own, 'seq')]
    dot_general x23 -> x0, matrix products: 64.9 us -> none  [the longest x1 9.54 us: body(): jnp.einsum('nthd,nhrd->nthr', grad_num, state, precision=HIGHEST)]
    reduce_sum x6 -> x1, other arithmetic: 19.2 us -> 1.03 us  [body(): own = head[1][0] + jnp.sum(rest[1], 0)]
    convert_element_type x6 -> x0, other arithmetic: 10.8 us -> none  [the longest x1 7.24 us: body(): return (out.astype(jnp.bfloat16)[None], grad_q, grad_k)]
    unnamed x93 -> x14, local copies, waits for them, and re-layouts: 11.3 us -> 1.65 us
    transpose x3 -> x0, local copies, waits for them, and re-layouts: 9.55 us -> none  [the longest x1 4.55 us: body(): jnp.einsum('nthr,nhrd->nthd', feat_qt, state, precision=HIGHEST)]
  transfers between devices with their start and end apart: 3 -> 5, of which waited for: 1 -> 3; matrix products, arithmetic and copies ran while one was open for 6% -> 2% of each run, Pallas kernels for 0% -> 15%
where the time goes in v1:
time: 320 us; the launch traced here: 319 us
  waiting for transfers between devices  195 us (61%)
  Pallas kernels  89.5 us (28%)
  between operations  13.9 us (4%)
  starting transfers between devices  8.48 us (3%)
  other arithmetic  7.17 us (2%)
  local copies, waits for them, and re-layouts  5.34 us (2%)
    psum x1, waiting for transfers between devices, body(): grads = lax.psum(grads, ('seq', 'batch'))  122 us
    pallas_call x2, Pallas kernels, attend(): pl.pallas_call(functools.partial(main_kernel, first, halo), name='attend_...  66.7 us
    all_gather x1, waiting for transfers between devices, body(): after = lax.all_gather(own, 'seq')  38.3 us
    all_gather x1, waiting for transfers between devices, body(): states = lax.all_gather(total, 'seq')  35 us
    pallas_call x1, Pallas kernels, local_states(): pl.pallas_call(state_kernel, name='local_states', grid=(tokens // TILE,),...  16.3 us
    ppermute x2, starting transfers between devices, body(): lax.ppermute((k_rows[tokens - TILE:], v_rows[tokens - TILE:]), 'seq', ring)  8.36 us
    pallas_call x1, Pallas kernels, key_grads(): pl.pallas_call(key_kernel, name='key_grads', grid=(heads // group,), in_s...  6.44 us
  transfers between devices with their start and end apart: 5, of which 3 were waited for; matrix products, arithmetic and copies ran while one was open for 2% of the time, Pallas kernels for 15%

profile of v1, /device:TPU:0, one launch (start us, length us, event | category | flops | bytes accessed | tf_op | source)
XLA Modules:
  0.0 319.5 jit_solution(11627854054853743304)
XLA Ops:
  7.2 0.0 all-gather.6.cloned.1.call-start
  7.2 16.3 %local_states.1 = (bf16[16,512,128]{2,1,0:T(8,128)(2,1)}, bf16[16,512,128]{2,1,0:T(8,128)(2,1)}, f32[16,8,256]{2,1,0:T(8,128)}) custom-call(bf16[512,16,128]{2,1,0:T(8,128)(2,1)} %bitcast.33, bf16[512,16,128]{2,1,0:T(8,128)(2,1)} %bitcast.34, bf16[16,8,128]{2,1,0:T(8,128)(2,1)} %bitcast.35), custom_call_target="tpu_custom_call" | custom-call | flops 1000000000 | bytes 8388608 | tf_op jit(solution)/shard_map/local_states/pallas_call | solution.py:86
  23.5 0.0 all-gather.4.cloned.1.call-start
  23.6 1.1 slice_bitcast_fusion.1
  24.7 4.9 %collective-permute-start = (bf16[128,16,128]{2,1,0:T(8,128)(2,1)S(1)}, bf16[128,16,128]{2,1,0:T(8,128)(2,1)S(1)}, u32[]{:S(2)}, u32[]{:S(2)}) collective-permute-start(bf16[128,16,128]{2,1,0:T(8,128)(2,1)S(1)} %slice_bitcast_fusion.1), channel_id=1, source_target_pairs={{0,4},{4,8},{8,12},{12,16},{16,20},{20,24},{24,28},{1,5},{5,9},{9,... | collective-permute-start | bytes 1572872 | tf_op jit(solution)/shard_map/ppermute | solution.py:278
  29.6 1.1 slice_bitcast_fusion
  30.7 3.4 %collective-permute-start.1 = (bf16[128,16,128]{2,1,0:T(8,128)(2,1)S(1)}, bf16[128,16,128]{2,1,0:T(8,128)(2,1)S(1)}, u32[]{:S(2)}, u32[]{:S(2)}) collective-permute-start(bf16[128,16,128]{2,1,0:T(8,128)(2,1)S(1)} %slice_bitcast_fusion), channel_id=1, source_target_pairs={{0,4},{4,8},{8,12},{12,16},{16,20},{20,24},{24,28},{1,5},{5,9},{9,... | collective-permute-start | bytes 1572872 | tf_op jit(solution)/shard_map/ppermute | solution.py:278
  34.1 0.7 pad_add_fusion.where_ref
  34.8 35.0 %all-gather.6.cloned.1.call-done = f32[128,8,256]{2,1,0:T(8,128)} async-done(((f32[16,8,256]{2,1,0:T(8,128)}), f32[128,8,256]{2,1,0:T(8,128)}) %all-gather.6.cloned.1.call-update) | async-done | bytes 1048592 | tf_op jit(solution)/shard_map/all_gather | solution.py:282
  69.8 48.4 %attend_rest.1 = (bf16[384,16,128]{2,1,0:T(8,128)(2,1)}, f32[3,16,8,256]{3,2,1,0:T(8,128)}, f32[16,8,128]{2,1,0:T(8,128)}, f32[16,8,128]{2,1,0:T(8,128)}) custom-call(s32[16,32]{1,0:T(8,128)} %bitcast.41, s32[2]{0:T(128)} %pad_add_fusion.where_ref, bf16[512,16,128]{2,1,0:T(8,128)(2,1)} %bitcast.27, ...), custom_call_target="tpu_custom_call" | custom-call | flops 3000000000 | bytes 12582912 | tf_op jit(solution)/shard_map/attend_rest/pallas_call | solution.py:200
  118.2 1.0 reduce_sum.11
  119.2 0.8 copy-done.1
  120.1 0.8 copy-done.2
  120.9 18.4 %attend_first.1 = (bf16[128,16,128]{2,1,0:T(8,128)(2,1)}, f32[1,16,8,256]{3,2,1,0:T(8,128)}, f32[16,8,128]{2,1,0:T(8,128)}, f32[16,8,128]{2,1,0:T(8,128)}) custom-call(s32[16,32]{1,0:T(8,128)} %bitcast.42, s32[2]{0:T(128)} %pad_add_fusion.where_ref, bf16[512,16,128]{2,1,0:T(8,128)(2,1)} %bitcast.28, ...), custom_call_target="tpu_custom_call" | custom-call | flops 1000000000 | bytes 4194304 | tf_op jit(solution)/shard_map/attend_first/pallas_call | solution.py:200
  139.3 1.6 bitcast_add_fusion
  140.9 0.0 all-reduce.2.cloned.1.call-start
  140.9 0.8 add_bitcast_fusion.1
  141.8 38.3 %all-gather.4.cloned.1.call-done.after_ref = f32[8,16,8,256]{3,2,1,0:T(8,128)} async-done(((f32[1,16,8,256]{3,2,1,0:T(8,128)}), f32[8,16,8,256]{3,2,1,0:T(8,128)}) %all-gather.4.cloned.1.call-update) | async-done | bytes 1048592 | tf_op jit(solution)/shard_map/all_gather | solution.py:286
  180.1 6.4 %key_grads.1 = f32[16,8,128]{2,1,0:T(8,128)} custom-call(s32[2]{0:T(128)} %pad_add_fusion.where_ref, bf16[16,512,128]{2,1,0:T(8,128)(2,1)} %get-tuple-element.14.k_ref.kp_ref.kh_ref, bf16[16,512,128]{2,1,0:T(8,128)(2,1)} %get-tuple-element.15.v_ref.vp_ref.vh_ref, bf16[16,8,128]{2,1,0:T(8,128)(2,1)} %bitcast.38, f32[1,16,8,256]{3,2,1,0:T(8,128)} %get-tuple-element.23.ds0_ref, ...), custom_call_target="tpu_custom_call" | custom-call | flops 1000000000 | bytes 8388608 | tf_op jit(solution)/shard_map/key_grads/pallas_call | solution.py:255
  186.5 0.9 add_bitcast_fusion
  187.4 0.7 maximum_bitcast_fusion.1
  188.1 1.5 maximum_bitcast_fusion
  189.6 121.8 %all-reduce.2.cloned.1.call-done = f32[2,16,128,8]{2,3,1,0:T(8,128)} async-done(((f32[2,16,128,8]{2,3,1,0:T(8,128)}), f32[2,16,128,8]{2,3,1,0:T(8,128)}) %all-reduce.2.cloned.1.call-update) | async-done | bytes 131088 | tf_op jit(solution)/shard_map/psum | solution.py:289
  311.4 1.5 slice_bitcast_fusion.2
  (17 shorter events, 0.1 us)
Async XLA Ops:
  7.2 62.6 %all-gather.6.cloned.1.call-start = ((), (), s32[]{:S(2)}) async-start(), calls=%async_computation.2 | async-start | bytes 1179648 | tf_op jit(solution)/shard_map/all_gather | solution.py:282
  23.5 156.6 %all-gather.4.cloned.1.call-start = ((), (), s32[]{:S(2)}) async-start(), calls=%async_computation | async-start | bytes 1179648 | tf_op jit(solution)/shard_map/all_gather | solution.py:286
  24.7 94.6 %collective-permute-start = (bf16[128,16,128]{2,1,0:T(8,128)(2,1)S(1)}, bf16[128,16,128]{2,1,0:T(8,128)(2,1)S(1)}, u32[]{:S(2)}, u32[]{:S(2)}) collective-permute-start(bf16[128,16,128]{2,1,0:T(8,128)(2,1)S(1)} %slice_bitcast_fusion.1), channel_id=1, source_target_pairs={{0,4},{4,8},{8,12},{12,16},{16,20},{20,24},{24,28},{1,5},{5,9},{9,... | collective-permute-start | bytes 1572872 | tf_op jit(solution)/shard_map/ppermute | solution.py:278
  30.7 88.6 %collective-permute-start.1 = (bf16[128,16,128]{2,1,0:T(8,128)(2,1)S(1)}, bf16[128,16,128]{2,1,0:T(8,128)(2,1)S(1)}, u32[]{:S(2)}, u32[]{:S(2)}) collective-permute-start(bf16[128,16,128]{2,1,0:T(8,128)(2,1)S(1)} %slice_bitcast_fusion), channel_id=1, source_target_pairs={{0,4},{4,8},{8,12},{12,16},{16,20},{20,24},{24,28},{1,5},{5,9},{9,... | collective-permute-start | bytes 1572872 | tf_op jit(solution)/shard_map/ppermute | solution.py:278
  119.2 21.7 %copy-start.4 = (f32[16,8,128]{2,1,0:T(8,128)S(1)}, f32[16,8,128]{2,1,0:T(8,128)}, u32[]{:S(2)}) copy-start(f32[16,8,128]{2,1,0:T(8,128)} %get-tuple-element.20) | copy-start | bytes 196612
  119.2 0.8 copy-start.1
  120.1 0.8 copy-start.2
  140.9 170.5 %all-reduce.2.cloned.1.call-start = ((), (), s32[]{:S(2)}) async-start(), calls=%async_computation.1 | async-start | bytes 262144 | tf_op jit(solution)/shard_map/psum | solution.py:289
  141.8 44.7 %copy-start.5 = (f32[16,8,128]{2,1,0:T(8,128)S(1)}, f32[16,8,128]{2,1,0:T(8,128)}, u32[]{:S(2)}) copy-start(f32[16,8,128]{2,1,0:T(8,128)} %get-tuple-element.22) | copy-start | bytes 196612
  141.8 44.7 %copy-start.6 = (f32[16,8,128]{2,1,0:T(8,128)S(1)}, f32[16,8,128]{2,1,0:T(8,128)}, u32[]{:S(2)}) copy-start(f32[16,8,128]{2,1,0:T(8,128)} %get-tuple-element.21) | copy-start | bytes 196612
  141.8 46.3 %copy-start = (bf16[384,16,128]{2,1,0:T(8,128)(2,1)S(1)}, bf16[384,16,128]{2,1,0:T(8,128)(2,1)}, u32[]{:S(2)}) copy-start(bf16[384,16,128]{2,1,0:T(8,128)(2,1)} %get-tuple-element.18) | copy-start | bytes 4718596
  141.8 46.3 %copy-start.3 = (bf16[128,16,128]{2,1,0:T(8,128)(2,1)S(1)}, bf16[128,16,128]{2,1,0:T(8,128)(2,1)}, u32[]{:S(2)}) copy-start(bf16[128,16,128]{2,1,0:T(8,128)(2,1)} %get-tuple-element.17) | copy-start | bytes 1572868
Sparse Core Ops, SparseCore 0:
  23.7 46.1 all-gather.5
  141.0 39.0 all-gather.3
  188.2 123.1 all-reduce.1

commit v2 on v1

--- a/solution.py
+++ b/solution.py
@@ -14,6 +14,7 @@
 MASKED = -1e30
 F32 = jnp.float32
 BF16 = jnp.bfloat16
+GROUP = 4
 VMEM_LIMIT = 56 * 1024 * 1024
 
 
@@ -66,12 +67,10 @@
     def _():
         acc_ref[...] = jnp.zeros_like(acc_ref)
 
-    def one_head(h, carry):
-        feat = softplus(dot_nt(wk_ref[h], kh_ref[h]) - SHIFT)
-        acc_ref[h] += split_dot(dot_nn, feat, with_ones(vh_ref[h]))
-        return carry
-
-    lax.fori_loop(0, heads, one_head, 0, unroll=4)
+    pre = jnp.stack([dot_nt(wk_ref[h], kh_ref[h]) for h in range(heads)], 0)
+    feat = softplus(pre - SHIFT)
+    for h in range(heads):
+        acc_ref[h] += split_dot(dot_nn, feat[h], with_ones(vh_ref[h]))
 
     @pl.when(step == pl.num_programs(0) - 1)
     def _():
@@ -106,7 +105,6 @@
 ):
     step = pl.program_id(0)
     heads = wq_ref.shape[0]
-    peers = states_ref.shape[0]
     width = q_ref.shape[2]
     me = where_ref[0]
     tiles_dev = where_ref[1]
@@ -123,10 +121,7 @@
     def _():
         gq_ref[...] = jnp.zeros_like(gq_ref)
         gk_ref[...] = jnp.zeros_like(gk_ref)
-        before = jnp.zeros(run.shape, F32)
-        for peer in range(peers):
-            before += jnp.where(peer < me, states_ref[peer].astype(F32), 0.0)
-        run[...] = before
+        run[...] = states_ref[...]
 
     tile = me * tiles_dev + first + step
     lane = lax.broadcasted_iota(jnp.int32, (1, TILE), 1)
@@ -134,54 +129,70 @@
     col = lax.broadcasted_iota(jnp.int32, (TILE, TILE), 1)
     causal = col <= row
 
-    def one_head(h, carry):
-        q, c = qh[h], ch[h]
-        k, v = k_ref[h], v_ref[h]
-        kp, vp = prev_k[h], prev_v[h]
-        count = jnp.where(tile > 0, counts_ref[h, jnp.maximum(tile - 1, 0)], 0)
-        kept = lane < count
-        kept_f = kept.astype(F32)
-        pre_p = dot_nt(wk_ref[h], kp) - SHIFT
-        feat_p = softplus(pre_p)
-        vp_ext = with_ones(vp)
-        rank = feat_p.shape[0]
-        both = split_dot(dot_nn, jnp.concatenate([feat_p, feat_p * kept_f], 0), vp_ext)
-        if halo:
-            state = run[h] - both[rank:]
-        else:
-            total = run[h] + both[:rank]
-            run[h] = total
-            state = total - both[rank:]
-        own = jnp.where(causal, dot_nt(q, k), MASKED)
-        old = jnp.where(kept, dot_nt(q, kp), MASKED)
-        top = jnp.max(jnp.maximum(own, old), 1, keepdims=True) * factor
-        p_own = jnp.exp2(own * factor - top).astype(BF16)
-        p_old = jnp.exp2(old * factor - top).astype(BF16)
-        numer = dot_nn(p_own, with_ones(v)) + dot_nn(p_old, vp_ext)
-        decay = jnp.exp2(-top)
-        pre_q = dot_nt(wq_ref[h], q) - SHIFT
-        feat_q = softplus(pre_q)
-        fq_top, fq_low = halves(feat_q)
-        st_top, st_low = halves(state)
-        kernel = dot_tn(jnp.concatenate([fq_top, fq_low, fq_top], 0), jnp.concatenate([st_top, st_top, st_low], 0))
-        full = numer + decay * kernel
-        inv = 1.0 / full[:, width:]
-        out = full[:, :width] * inv
-        oh[h] = out.astype(BF16)
-        gn = decay * (c.astype(F32) * inv)
-        g_ext = jnp.concatenate([gn, gn * out], 1).astype(BF16)
-        signed = jnp.concatenate([state[:, :width], -state[:, width:]], 1)
-        dpre_q = split_dot(dot_nt, signed, g_ext) * sigmoid(pre_q)
-        gq_ref[h] += split_dot(dot_nn, dpre_q, q)
-        ds = split_dot(dot_nn, feat_q, g_ext)
-        ds_ref[0, h] = ds
-        dn = -jnp.sum(ds[:, width:], 1, keepdims=True)
-        dfk = split_dot(dot_nt, ds[:, :width], vp) + dn
-        dpre_k = -kept_f * dfk * sigmoid(pre_p)
-        gk_ref[h] += split_dot(dot_nn, dpre_k, kp)
+    def some_heads(g, carry):
+        hs = [g * GROUP + i for i in range(GROUP)]
+        each = range(GROUP)
+        qs, ks, vs = [qh[h] for h in hs], [k_ref[h] for h in hs], [v_ref[h] for h in hs]
+        kps, vps = [prev_k[h] for h in hs], [prev_v[h] for h in hs]
+        own_raw = [dot_nt(qs[i], ks[i]) for i in each]
+        old_raw = [dot_nt(qs[i], kps[i]) for i in each]
+        pre_p = [dot_nt(wk_ref[hs[i]], kps[i]) - SHIFT for i in each]
+        pre_q = [dot_nt(wq_ref[hs[i]], qs[i]) - SHIFT for i in each]
+        counts = [jnp.where(tile > 0, counts_ref[h, jnp.maximum(tile - 1, 0)], 0) for h in hs]
+        kept = [lane < count for count in counts]
+        kept_f = [keep.astype(F32) for keep in kept]
+        own = [jnp.where(causal, own_raw[i], MASKED) for i in each]
+        old = [jnp.where(kept[i], old_raw[i], MASKED) for i in each]
+        top = [jnp.max(jnp.maximum(own[i], old[i]), 1, keepdims=True) * factor for i in each]
+        feat_p = [softplus(pre) for pre in pre_p]
+        feat_q = [softplus(pre) for pre in pre_q]
+        both = [
+            split_dot(dot_nn, jnp.concatenate([feat_p[i], feat_p[i] * kept_f[i]], 0), with_ones(vps[i])) for i in each
+        ]
+        state = []
+        for i in each:
+            rank = feat_p[i].shape[0]
+            total = run[hs[i]]
+            if not halo:
+                total += both[i][:rank]
+                run[hs[i]] = total
+            state.append(total - both[i][rank:])
+        p_own = [jnp.exp2(own[i] * factor - top[i]).astype(BF16) for i in each]
+        p_old = [jnp.exp2(old[i] * factor - top[i]).astype(BF16) for i in each]
+        numer = [dot_nn(p_own[i], with_ones(vs[i])) + dot_nn(p_old[i], with_ones(vps[i])) for i in each]
+        decay = [jnp.exp2(-t) for t in top]
+        kernel = []
+        for i in each:
+            fq_top, fq_low = halves(feat_q[i])
+            st_top, st_low = halves(state[i])
+            kernel.append(
+                dot_tn(jnp.concatenate([fq_top, fq_low, fq_top], 0), jnp.concatenate([st_top, st_top, st_low], 0))
+            )
+        g_ext = []
+        for i in each:
+            full = numer[i] + decay[i] * kernel[i]
+            inv = 1.0 / full[:, width:]
+            out = full[:, :width] * inv
+            oh[hs[i]] = out.astype(BF16)
+            gn = decay[i] * (ch[hs[i]].astype(F32) * inv)
+            g_ext.append(jnp.concatenate([gn, gn * out], 1).astype(BF16))
+        signed = [jnp.concatenate([st[:, :width], -st[:, width:]], 1) for st in state]
+        d_fq = [split_dot(dot_nt, signed[i], g_ext[i]) for i in each]
+        ds = [split_dot(dot_nn, feat_q[i], g_ext[i]) for i in each]
+        dpre_q = [d_fq[i] * sigmoid(pre_q[i]) for i in each]
+        d_fk = [
+            split_dot(dot_nt, ds[i][:, :width], vps[i]) - jnp.sum(ds[i][:, width:], 1, keepdims=True) for i in each
+        ]
+        dpre_k = [-kept_f[i] * d_fk[i] * sigmoid(pre_p[i]) for i in each]
+        gq = [split_dot(dot_nn, dpre_q[i], qs[i]) for i in each]
+        gk = [split_dot(dot_nn, dpre_k[i], kps[i]) for i in each]
+        for i in each:
+            ds_ref[0, hs[i]] = ds[i]
+            gq_ref[hs[i]] += gq[i]
+            gk_ref[hs[i]] += gk[i]
         return carry
 
-    lax.fori_loop(0, heads, one_head, 0, unroll=4)
+    lax.fori_loop(0, heads // GROUP, some_heads, 0)
     out_ref[...] = by_head(oh[...])
 
 
@@ -203,7 +214,7 @@
         grid=(steps,),
         in_specs=[
             smem, smem, row_spec, head_spec, head_spec, prev_spec, prev_spec, row_spec, whole, whole,
-            pl.BlockSpec(states.shape, lambda n: (0, 0, 0, 0)),
+            pl.BlockSpec(states.shape, lambda n: (0, 0, 0)),
         ],
         out_specs=[
             pl.BlockSpec((TILE, heads, width), lambda n: (n, 0, 0)),
@@ -223,47 +234,256 @@
     )(counts, where, q_rows, kh, vh, kp, vp, cot, wq, wk, states)
 
 
-def key_kernel(where_ref, kh_ref, vh_ref, wk_ref, ds0_ref, ds1_ref, after_ref, gk_ref):
+def key_kernel(kh_ref, vh_ref, wk_ref, ds1_ref, after_ref, gk_ref):
     group, tokens, width = kh_ref.shape
     tiles = tokens // TILE
-    me = where_ref[0]
-    for h in range(group):
-        later = jnp.zeros(ds0_ref.shape[2:], F32)
-        for peer in range(after_ref.shape[0]):
-            later += jnp.where(peer > me, after_ref[peer, h].astype(F32), 0.0)
-        pre = dot_nt(wk_ref[h], kh_ref[h]) - SHIFT
+    each = range(group)
+    pre = [dot_nt(wk_ref[h], kh_ref[h]) - SHIFT for h in each]
+    grads = []
+    for h in each:
+        later = after_ref[h][:, :width]
+        norm = after_ref[h][:, width:]
         pieces = [None] * tiles
         for n in reversed(range(tiles)):
-            dn = -jnp.sum(later[:, width:], 1, keepdims=True)
-            pieces[n] = split_dot(dot_nt, later[:, :width], vh_ref[h, n * TILE : (n + 1) * TILE]) + dn
+            pieces[n] = split_dot(dot_nt, later, vh_ref[h, n * TILE : (n + 1) * TILE]) + norm
             if n:
-                later += ds1_ref[n - 1, h]
-        grad = jnp.concatenate(pieces, 1) * sigmoid(pre)
-        gk_ref[h] = split_dot(dot_nn, grad, kh_ref[h])
-
-
-def key_grads(where, kh, vh, wk, ds0, ds1, after):
+                later += ds1_ref[n - 1, h][:, :width]
+                norm -= jnp.sum(ds1_ref[n - 1, h][:, width:], 1, keepdims=True)
+        grads.append(jnp.concatenate(pieces, 1))
+    for h in each:
+        gk_ref[h] = split_dot(dot_nn, grads[h] * sigmoid(pre[h]), kh_ref[h])
+
+
+def flat_id(axes):
+    index, count = 0, 1
+    for axis in axes:
+        index = index * lax.axis_size(axis) + lax.axis_index(axis)
+        count *= lax.axis_size(axis)
+    return index, count
+
+
+def place(flat, axes):
+    where = {}
+    for axis in reversed(axes):
+        size = lax.axis_size(axis)
+        where[axis] = lax.rem(flat, size)
+        flat = flat // size
+    return where
+
+
+def greet(count, me, axes):
+    barrier = pltpu.get_barrier_semaphore()
+
+    def hello(i, carry):
+        pl.semaphore_signal(
+            barrier, inc=1, device_id=place(lax.rem(me + i, count), axes), device_id_type=pl.DeviceIdType.MESH
+        )
+        return carry
+
+    lax.fori_loop(1, count, hello, 0)
+    return barrier
+
+
+def others_kernel(axis, later, *refs):
+    parts, (out_ref, mine, slots, send_sem, recv_sem) = refs[:-5], refs[-5:]
+    heads, _, twice = out_ref.shape
+    width = twice // 2
+    axes = (axis,)
+    me, count = flat_id(axes)
+    barrier = greet(count, me, axes)
+    lane = lax.broadcasted_iota(jnp.int32, (1, width), 1)
+    packed = jnp.zeros(mine.shape[1:], F32)
+    for h in range(heads):
+        own = sum(part[n, h] for part in parts for n in range(part.shape[0]))
+        mine[h] = own[:, :width]
+        norm = -jnp.sum(own[:, width:], 1, keepdims=True) if later else own[:, width:]
+        packed = jnp.where(lane == h, norm, packed)
+    mine[heads] = packed
+    pl.semaphore_wait(barrier, count - 1)
+
+    def copy(sender, target):
+        return pltpu.make_async_remote_copy(
+            src_ref=mine,
+            dst_ref=slots.at[sender],
+            send_sem=send_sem.at[target],
+            recv_sem=recv_sem.at[sender],
+            device_id=place(target, axes),
+            device_id_type=pl.DeviceIdType.MESH,
+        )
+
+    slots[me] = jnp.zeros(mine.shape, F32)
+    if later:
+        first_to, end_to, first_from, end_from = 0, me, me + 1, count
+    else:
+        first_to, end_to, first_from, end_from = me + 1, count, 0, me
+
+    def send(p, carry):
+        copy(me, p).start()
+        return carry
+
+    def sent(p, carry):
+        copy(me, p).wait_send()
+        return carry
+
+    def received(p, total):
+        copy(p, lax.rem(me + 1, count)).wait_recv()
+        return total + slots[p]
+
+    lax.fori_loop(first_to, end_to, send, 0)
+    total = lax.fori_loop(first_from, end_from, received, jnp.zeros(mine.shape, F32))
+    lax.fori_loop(first_to, end_to, sent, 0)
+    for h in range(heads):
+        norm = jnp.sum(jnp.where(lane == h, total[heads], 0.0), 1, keepdims=True)
+        out_ref[h] = jnp.concatenate([total[h], jnp.broadcast_to(norm, total[h].shape)], 1)
+
+
+def sum_of_others(parts, axis, later, collective_id):
+    heads, rank, twice = parts[0].shape[1:]
+    count = lax.axis_size(axis)
+    block = (heads + 1, rank, twice // 2)
+    vmem = pl.BlockSpec(memory_space=pltpu.VMEM)
+    return pl.pallas_call(
+        functools.partial(others_kernel, axis, later),
+        name="later_grads" if later else "earlier_states",
+        in_specs=[vmem] * len(parts),
+        out_specs=vmem,
+        out_shape=jax.ShapeDtypeStruct((heads, rank, twice), F32),
+        scratch_shapes=[
+            pltpu.VMEM(block, F32),
+            pltpu.VMEM((count,) + block, F32),
+            pltpu.SemaphoreType.DMA((count,)),
+            pltpu.SemaphoreType.DMA((count,)),
+        ],
+        compiler_params=pltpu.CompilerParams(
+            collective_id=collective_id, has_side_effects=True, vmem_limit_bytes=VMEM_LIMIT
+        ),
+        cost_estimate=pl.CostEstimate(flops=10**7, bytes_accessed=2**20, transcendentals=0),
+    )(*parts)
+
+
+def reduce_kernel(axes, gq0, gq1, gk0, gk1, gk2, out_ref, mine, slots, done, out_sem, in_sem, back_sem, res_sem):
+    heads = gq0.shape[0]
+    chunks = 2 * heads
+    me, count = flat_id(axes)
+    owners = min(count, chunks)
+    stride, per = count // owners, chunks // owners
+    barrier = greet(count, me, axes)
+    mine[:heads] = gq0[...] + gq1[...]
+    mine[heads:] = gk0[...] + gk1[...] + gk2[...]
+    pl.semaphore_wait(barrier, count - 1)
+    owner = lax.rem(me, stride) == 0
+    part = me // stride
+
+    def to_owner(o, sender):
+        return pltpu.make_async_remote_copy(
+            src_ref=mine.at[pl.ds(o * per, per)],
+            dst_ref=slots.at[sender],
+            send_sem=out_sem.at[o],
+            recv_sem=in_sem.at[sender],
+            device_id=place(o * stride, axes),
+            device_id_type=pl.DeviceIdType.MESH,
+        )
+
+    def to_all(o, target):
+        return pltpu.make_async_remote_copy(
+            src_ref=done.at[pl.ds(o * per, per)],
+            dst_ref=done.at[pl.ds(o * per, per)],
+            send_sem=back_sem.at[target],
+            recv_sem=res_sem.at[o],
+            device_id=place(target, axes),
+            device_id_type=pl.DeviceIdType.MESH,
+        )
+
+    def over_owners(act):
+        def step(i, carry):
+            o = lax.rem(part + i, owners)
+
+            @pl.when(o * stride != me)
+            def _():
+                act(o)
+
+            return carry
+
+        lax.fori_loop(0, owners, step, 0)
+
+    over_owners(lambda o: to_owner(o, me).start())
+
+    @pl.when(owner)
+    def _():
+        def arrived(i, total):
+            sender = lax.rem(me + i, count)
+            to_owner(part, sender).wait_recv()
+            return total + slots[sender]
+
+        done[pl.ds(part * per, per)] = lax.fori_loop(1, count, arrived, mine[pl.ds(part * per, per)])
+
+        def send(i, carry):
+            to_all(part, lax.rem(me + i, count)).start()
+            return carry
+
+        lax.fori_loop(1, count, send, 0)
+
+    over_owners(lambda o: to_owner(o, me).wait_send())
+    over_owners(lambda o: to_all(o, lax.rem(me + 1, count)).wait_recv())
+
+    @pl.when(owner)
+    def _():
+        def sent(i, carry):
+            to_all(part, lax.rem(me + i, count)).wait_send()
+            return carry
+
+        lax.fori_loop(1, count, sent, 0)
+
+    out_ref[...] = done[...]
+
+
+def sum_over_all(grads, axes):
+    heads, rank, width = grads[0].shape
+    count = math.prod(lax.axis_size(axis) for axis in axes)
+    owners = min(count, 2 * heads)
+    per = 2 * heads // owners
+    vmem = pl.BlockSpec(memory_space=pltpu.VMEM)
+    whole = (2 * heads, rank, width)
+    return pl.pallas_call(
+        functools.partial(reduce_kernel, axes),
+        name="sum_grads",
+        in_specs=[vmem] * len(grads),
+        out_specs=vmem,
+        out_shape=jax.ShapeDtypeStruct(whole, F32),
+        scratch_shapes=[
+            pltpu.VMEM(whole, F32),
+            pltpu.VMEM((count, per, rank, width), F32),
+            pltpu.VMEM(whole, F32),
+            pltpu.SemaphoreType.DMA((owners,)),
+            pltpu.SemaphoreType.DMA((count,)),
+            pltpu.SemaphoreType.DMA((count,)),
+            pltpu.SemaphoreType.DMA((owners,)),
+        ],
+        compiler_params=pltpu.CompilerParams(collective_id=2, has_side_effects=True, vmem_limit_bytes=VMEM_LIMIT),
+        cost_estimate=pl.CostEstimate(flops=10**7, bytes_accessed=2**20, transcendentals=0),
+    )(*grads)
+
+
+def key_grads(kh, vh, wk, ds1, after):
     heads, tokens, width = kh.shape
     rank = wk.shape[1]
     group = 4
     head_spec = pl.BlockSpec((group, tokens, width), lambda n: (n, 0, 0))
     whole = pl.BlockSpec((group, rank, width), lambda n: (n, 0, 0))
-
-    def four(a):
-        return pl.BlockSpec((a.shape[0], group) + a.shape[2:], lambda n: (0, n, 0, 0))
+    four = pl.BlockSpec((ds1.shape[0], group, rank, 2 * width), lambda n: (0, n, 0, 0))
 
     return pl.pallas_call(
         key_kernel,
         name="key_grads",
         grid=(heads // group,),
         in_specs=[
-            pl.BlockSpec(memory_space=pltpu.SMEM), head_spec, head_spec, whole, four(ds0), four(ds1), four(after),
+            head_spec, head_spec, whole, four, pl.BlockSpec((group, rank, 2 * width), lambda n: (n, 0, 0)),
         ],
         out_specs=whole,
         out_shape=jax.ShapeDtypeStruct((heads, rank, width), F32),
         compiler_params=pltpu.CompilerParams(vmem_limit_bytes=VMEM_LIMIT),
         cost_estimate=pl.CostEstimate(flops=10**9, bytes_accessed=8 * 2**20, transcendentals=10**6),
-    )(where, kh, vh, wk, ds0, ds1, after)
+    )(kh, vh, wk, ds1, after)
 
 
 def body(queries, keys, values, keep_count, query_map, key_map, cotangent):
@@ -279,15 +499,14 @@
     wq = jnp.swapaxes(query_map, 1, 2)
     wk = jnp.swapaxes(key_map, 1, 2)
     kh, vh, total = local_states(k_rows, v_rows, wk)
-    states = lax.all_gather(total, "seq")
+    states = sum_of_others([total[None]], "seq", False, 0)
     rest = attend(1, tiles - 1, False, counts, where, q_rows, kh, vh, kh, vh, cot, wq, wk, states)
     head = attend(0, 1, True, counts, where, q_rows, kh, vh, kp, vp, cot, wq, wk, states)
-    own = head[1][0] + jnp.sum(rest[1], 0)
-    after = lax.all_gather(own, "seq")
-    gk = key_grads(where, kh, vh, wk, head[1], rest[1], after)
-    grads = jnp.stack([head[2] + rest[2], head[3] + rest[3] + gk])
-    grads = lax.psum(grads, ("seq", "batch"))
-    grads = jnp.swapaxes(grads, 2, 3)
+    after = sum_of_others([head[1], rest[1]], "seq", True, 1)
+    gk = key_grads(kh, vh, wk, rest[1], after)
+    heads, rank, width = wq.shape
+    grads = sum_over_all([head[2], rest[2], head[3], rest[3], gk], ("seq", "batch"))
+    grads = jnp.swapaxes(grads.reshape(2, heads, rank, width), 2, 3)
     out = jnp.concatenate([head[0], rest[0]], 0)
     return out[None], grads[0], grads[1]
 

time: 320 us -> 115 us (0.36)
  waiting for transfers between devices: 195 us -> 0.01 us
  between operations: 13.9 us -> 0.73 us
  Pallas kernels: 89.5 us -> 98.1 us
  other arithmetic: 7.17 us -> 2.06 us
    psum x1 -> x0, waiting for transfers between devices: 122 us -> none  [body(): grads = lax.psum(grads, ('seq', 'batch'))]
    all_gather x2 -> x0, waiting for transfers between devices: 73.3 us -> none  [the longest x1 38.3 us: body(): after = lax.all_gather(own, 'seq')]
    pallas_call x0 -> x3, Pallas kernels: none -> 59.7 us  [the longest x2 39.2 us: sum_of_others(): pl.pallas_call(functools.partial(others_kernel, axis, later), name='later...]
    pallas_call x2, Pallas kernels: 66.7 us -> 26.8 us  [attend(): pl.pallas_call(functools.partial(main_kernel, first, halo), name='attend_...]
    pallas_call x1, Pallas kernels: 16.3 us -> 6.32 us  [local_states(): pl.pallas_call(state_kernel, name='local_states', grid=(tokens // TILE,),...]
  transfers between devices with their start and end apart: 5 -> 2, of which waited for: 3 -> 0; matrix products, arithmetic and copies ran while one was open for 2% -> 1% of each run, Pallas kernels for 15% -> 34%
where the time goes in v2:
time: 115 us
  Pallas kernels  98.1 us (85%)
  starting transfers between devices  8.36 us (7%)
  local copies, waits for them, and re-layouts  5.28 us (5%)
  other arithmetic  2.06 us (2%)
    pallas_call x2, Pallas kernels, sum_of_others(): pl.pallas_call(functools.partial(others_kernel, axis, later), name='later...  39.2 us
    pallas_call x2, Pallas kernels, attend(): pl.pallas_call(functools.partial(main_kernel, first, halo), name='attend_...  26.8 us
    pallas_call x1, Pallas kernels, sum_over_all(): pl.pallas_call(functools.partial(reduce_kernel, axes), name='sum_grads',...  20.5 us
    ppermute x2, starting transfers between devices, body(): lax.ppermute((k_rows[tokens - TILE:], v_rows[tokens - TILE:]), 'seq', ring)  8.36 us
    pallas_call x1, Pallas kernels, local_states(): pl.pallas_call(state_kernel, name='local_states', grid=(tokens // TILE,),...  6.32 us
    pallas_call x1, Pallas kernels, key_grads(): pl.pallas_call(key_kernel, name='key_grads', grid=(heads // group,), in_s...  5.27 us
  transfers between devices with their start and end apart: 2, of which 0 were waited for; matrix products, arithmetic and copies ran while one was open for 1% of the time, Pallas kernels for 34%

profile of v2, /device:TPU:0, one launch (start us, length us, event | category | flops | bytes accessed | tf_op | source)
XLA Modules:
  0.0 114.5 jit_solution(4563881414979817755)
XLA Ops:
  0.6 1.1 slice_bitcast_fusion
  1.7 4.9 %collective-permute-start.1 = (bf16[128,16,128]{2,1,0:T(8,128)(2,1)S(1)}, bf16[128,16,128]{2,1,0:T(8,128)(2,1)S(1)}, u32[]{:S(2)}, u32[]{:S(2)}) collective-permute-start(bf16[128,16,128]{2,1,0:T(8,128)(2,1)S(1)} %slice_bitcast_fusion), channel_id=1, source_target_pairs={{0,4},{4,8},{8,12},{12,16},{16,20},{20,24},{24,28},{1,5},{5,9},{9,... | collective-permute-start | bytes 1572872 | tf_op jit(solution)/shard_map/ppermute | solution.py:498
  6.7 1.1 slice_bitcast_fusion.1
  7.7 3.4 %collective-permute-start = (bf16[128,16,128]{2,1,0:T(8,128)(2,1)S(1)}, bf16[128,16,128]{2,1,0:T(8,128)(2,1)S(1)}, u32[]{:S(2)}, u32[]{:S(2)}) collective-permute-start(bf16[128,16,128]{2,1,0:T(8,128)(2,1)S(1)} %slice_bitcast_fusion.1), channel_id=1, source_target_pairs={{0,4},{4,8},{8,12},{12,16},{16,20},{20,24},{24,28},{1,5},{5,9},{9,... | collective-permute-start | bytes 1572872 | tf_op jit(solution)/shard_map/ppermute | solution.py:498
  11.2 6.3 %local_states.1 = (bf16[16,512,128]{2,1,0:T(8,128)(2,1)}, bf16[16,512,128]{2,1,0:T(8,128)(2,1)}, f32[16,8,256]{2,1,0:T(8,128)}) custom-call(bf16[512,16,128]{2,1,0:T(8,128)(2,1)} %bitcast.26, bf16[512,16,128]{2,1,0:T(8,128)(2,1)} %bitcast.27, bf16[16,8,128]{2,1,0:T(8,128)(2,1)} %bitcast.28), custom_call_target="tpu_custom_call" | custom-call | flops 1000000000 | bytes 8388608 | tf_op jit(solution)/shard_map/local_states/pallas_call | solution.py:85
  17.5 13.9 %earlier_states.1.states_ref = f32[16,8,256]{2,1,0:T(8,128)} custom-call(f32[1,16,8,256]{3,2,1,0:T(8,128)} %bitcast.35), custom_call_target="tpu_custom_call" | custom-call | flops 10000000 | bytes 1048576 | tf_op jit(solution)/shard_map/earlier_states/pallas_call | solution.py:345
  31.4 0.6 pad_add_fusion.where_ref
  32.0 18.6 %attend_rest.1 = (bf16[384,16,128]{2,1,0:T(8,128)(2,1)}, f32[3,16,8,256]{3,2,1,0:T(8,128)}, f32[16,8,128]{2,1,0:T(8,128)}, f32[16,8,128]{2,1,0:T(8,128)}) custom-call(s32[16,32]{1,0:T(8,128)} %bitcast.36, s32[2]{0:T(128)} %pad_add_fusion.where_ref, bf16[512,16,128]{2,1,0:T(8,128)(2,1)} %bitcast.22, ...), custom_call_target="tpu_custom_call" | custom-call | flops 3000000000 | bytes 12582912 | tf_op jit(solution)/shard_map/attend_rest/pallas_call | solution.py:211
  50.6 0.0 collective-permute-done.1.vp_ref
  50.6 0.0 copy-start.1
  50.6 0.0 collective-permute-done.kp_ref
  50.6 0.8 copy-done.1
  51.4 0.0 copy-start.2
  51.4 0.8 copy-done.2
  52.2 8.2 %attend_first.1 = (bf16[128,16,128]{2,1,0:T(8,128)(2,1)}, f32[1,16,8,256]{3,2,1,0:T(8,128)}, f32[16,8,128]{2,1,0:T(8,128)}, f32[16,8,128]{2,1,0:T(8,128)}) custom-call(s32[16,32]{1,0:T(8,128)} %bitcast.37, s32[2]{0:T(128)} %pad_add_fusion.where_ref, bf16[512,16,128]{2,1,0:T(8,128)(2,1)} %bitcast.23, ...), custom_call_target="tpu_custom_call" | custom-call | flops 1000000000 | bytes 4194304 | tf_op jit(solution)/shard_map/attend_first/pallas_call | solution.py:211
  60.4 25.3 %later_grads.1.after_ref = f32[16,8,256]{2,1,0:T(8,128)} custom-call(f32[1,16,8,256]{3,2,1,0:T(8,128)} %get-tuple-element.24.refs_0_, f32[3,16,8,256]{3,2,1,0:T(8,128)} %get-tuple-element.23.refs_1_.ds1_ref), custom_call_target="tpu_custom_call" | custom-call | flops 10000000 | bytes 1048576 | tf_op jit(solution)/shard_map/later_grads/pallas_call | solution.py:345
  85.6 0.0 copy-start
  85.6 0.0 copy-start.3
  85.7 5.3 %key_grads.1.gk2 = f32[16,8,128]{2,1,0:T(8,128)} custom-call(bf16[16,512,128]{2,1,0:T(8,128)(2,1)} %get-tuple-element.14.k_ref.kp_ref.kh_ref, bf16[16,512,128]{2,1,0:T(8,128)(2,1)} %get-tuple-element.15.v_ref.vp_ref.vh_ref, bf16[16,8,128]{2,1,0:T(8,128)(2,1)} %bitcast.31, f32[3,16,8,256]{3,2,1,0:T(8,128)} %get-tuple-element.23.refs_1_.ds1_ref, ...), custom_call_target="tpu_custom_call" | custom-call | flops 1000000000 | bytes 8388608 | tf_op jit(solution)/shard_map/key_grads/pallas_call | solution.py:475
  90.9 20.5 %sum_grads.1 = f32[32,8,128]{2,1,0:T(8,128)} custom-call(f32[16,8,128]{2,1,0:T(8,128)} %get-tuple-element.19.gq0, f32[16,8,128]{2,1,0:T(8,128)} %get-tuple-element.20.gq1, f32[16,8,128]{2,1,0:T(8,128)} %get-tuple-element.21.gk0, f32[16,8,128]{2,1,0:T(8,128)} %get-tuple-element.22.gk1, f32[16,8,128]{2,1,0:T(8,128)} %key_grads.1.gk2), custom_call_target="tpu_custom_call" | custom-call | flops 10000000 | bytes 1048576 | tf_op jit(solution)/shard_map/sum_grads/pallas_call | solution.py:447
  111.5 1.5 %slice_bitcast_fusion.2 = (f32[16,128,8]{1,2,0:T(8,128)}, f32[16,128,8]{1,2,0:T(8,128)}) fusion(f32[2,16,128,8]{2,3,1,0:T(8,128)} %bitcast.32), kind=kLoop, calls=%fused_computation.3 | loop fusion | bytes 262144 | tf_op jit(solution)/shard_map/squeeze | solution.py:511
  113.0 0.0 copy-done
  113.0 0.0 copy-done.3
  113.0 1.5 %maximum_bitcast_fusion = bf16[1,512,16,128]{3,2,1,0:T(8,128)(2,1)} fusion(bf16[384,16,128]{2,1,0:T(8,128)(2,1)S(1)} %copy-done, bf16[128,16,128]{2,1,0:T(8,128)(2,1)S(1)} %copy-done.3), kind=kLoop, calls=%fused_computation | loop fusion | flops 1048576 | bytes 4194304 | tf_op jit(solution)/shard_map/broadcast_in_dim | solution.py:511
Async XLA Ops:
  1.7 48.9 %collective-permute-start.1 = (bf16[128,16,128]{2,1,0:T(8,128)(2,1)S(1)}, bf16[128,16,128]{2,1,0:T(8,128)(2,1)S(1)}, u32[]{:S(2)}, u32[]{:S(2)}) collective-permute-start(bf16[128,16,128]{2,1,0:T(8,128)(2,1)S(1)} %slice_bitcast_fusion), channel_id=1, source_target_pairs={{0,4},{4,8},{8,12},{12,16},{16,20},{20,24},{24,28},{1,5},{5,9},{9,... | collective-permute-start | bytes 1572872 | tf_op jit(solution)/shard_map/ppermute | solution.py:498
  7.7 42.9 %collective-permute-start = (bf16[128,16,128]{2,1,0:T(8,128)(2,1)S(1)}, bf16[128,16,128]{2,1,0:T(8,128)(2,1)S(1)}, u32[]{:S(2)}, u32[]{:S(2)}) collective-permute-start(bf16[128,16,128]{2,1,0:T(8,128)(2,1)S(1)} %slice_bitcast_fusion.1), channel_id=1, source_target_pairs={{0,4},{4,8},{8,12},{12,16},{16,20},{20,24},{24,28},{1,5},{5,9},{9,... | collective-permute-start | bytes 1572872 | tf_op jit(solution)/shard_map/ppermute | solution.py:498
  50.6 0.8 copy-start.1
  51.4 0.8 copy-start.2
  85.6 27.4 %copy-start = (bf16[384,16,128]{2,1,0:T(8,128)(2,1)S(1)}, bf16[384,16,128]{2,1,0:T(8,128)(2,1)}, u32[]{:S(2)}) copy-start(bf16[384,16,128]{2,1,0:T(8,128)(2,1)} %get-tuple-element.18) | copy-start | bytes 4718596
  85.6 27.4 %copy-start.3 = (bf16[128,16,128]{2,1,0:T(8,128)(2,1)S(1)}, bf16[128,16,128]{2,1,0:T(8,128)(2,1)}, u32[]{:S(2)}) copy-start(bf16[128,16,128]{2,1,0:T(8,128)(2,1)} %get-tuple-element.17) | copy-start | bytes 1572868

commit v3 on v2

--- a/solution.py
+++ b/solution.py
@@ -14,7 +14,7 @@
 MASKED = -1e30
 F32 = jnp.float32
 BF16 = jnp.bfloat16
-GROUP = 4
+GROUP = 8
 VMEM_LIMIT = 56 * 1024 * 1024
 
 
@@ -101,8 +101,9 @@
 
 def main_kernel(
     first, halo, counts_ref, where_ref, q_ref, k_ref, v_ref, kp_ref, vp_ref, c_ref, wq_ref, wk_ref,
-    states_ref, out_ref, ds_ref, gq_ref, gk_ref, qh, ch, oh, kph, vph, run,
+    states_ref, *refs,
 ):
+    out_ref, ds_ref, gq_ref, gk_ref, qh, ch, oh, kph, vph, run = refs[-10:]
     step = pl.program_id(0)
     heads = wq_ref.shape[0]
     width = q_ref.shape[2]
@@ -196,15 +197,16 @@
     out_ref[...] = by_head(oh[...])
 
 
-def attend(first, steps, halo, counts, where, q_rows, kh, vh, kp, vp, cot, wq, wk, states):
+def attend(first, steps, begun, counts, where, q_rows, kh, vh, kp, vp, cot, wq, wk, states):
     tokens, heads, width = q_rows.shape
     rank = wq.shape[1]
     row_spec = pl.BlockSpec((TILE, heads, width), lambda n: (n + first, 0, 0))
     head_spec = pl.BlockSpec((heads, TILE, width), lambda n: (0, n + first, 0))
+    halo = begun is not None
     if halo:
-        prev_spec = pl.BlockSpec((TILE, heads, width), lambda n: (0, 0, 0))
+        prev_specs = [pl.BlockSpec((None, TILE, heads, width), lambda n, i=i: (i, 0, 0, 0)) for i in range(2)]
     else:
-        prev_spec = pl.BlockSpec((heads, TILE, width), lambda n: (0, n + first - 1, 0))
+        prev_specs = [pl.BlockSpec((heads, TILE, width), lambda n: (0, n + first - 1, 0))] * 2
     whole = pl.BlockSpec((heads, rank, width), lambda n: (0, 0, 0))
     smem = pl.BlockSpec(memory_space=pltpu.SMEM)
     tile_scratch = pltpu.VMEM((heads, TILE, width), BF16)
@@ -213,17 +215,17 @@
         name="attend_first" if halo else "attend_rest",
         grid=(steps,),
         in_specs=[
-            smem, smem, row_spec, head_spec, head_spec, prev_spec, prev_spec, row_spec, whole, whole,
+            smem, smem, row_spec, head_spec, head_spec, *prev_specs, row_spec, whole, whole,
             pl.BlockSpec(states.shape, lambda n: (0, 0, 0)),
-        ],
+        ] + [pl.BlockSpec(memory_space=pl.ANY)] * halo,
         out_specs=[
-            pl.BlockSpec((TILE, heads, width), lambda n: (n, 0, 0)),
+            row_spec,
             pl.BlockSpec((1, heads, rank, 2 * width), lambda n: (n, 0, 0, 0)),
             whole,
             whole,
         ],
         out_shape=[
-            jax.ShapeDtypeStruct((steps * TILE, heads, width), BF16),
+            jax.ShapeDtypeStruct((tokens, heads, width), BF16),
             jax.ShapeDtypeStruct((steps, heads, rank, 2 * width), F32),
             jax.ShapeDtypeStruct((heads, rank, width), F32),
             jax.ShapeDtypeStruct((heads, rank, width), F32),
@@ -231,7 +233,8 @@
         scratch_shapes=[tile_scratch] * 5 + [pltpu.VMEM((heads, rank, 2 * width), F32)],
         compiler_params=pltpu.CompilerParams(vmem_limit_bytes=VMEM_LIMIT),
         cost_estimate=pl.CostEstimate(flops=10**9 * steps, bytes_accessed=steps * 4 * 2**20, transcendentals=10**6),
-    )(counts, where, q_rows, kh, vh, kp, vp, cot, wq, wk, states)
+        input_output_aliases={11: 0} if halo else {},
+    )(counts, where, q_rows, kh, vh, kp, vp, cot, wq, wk, states, *([begun] if halo else []))
 
 
 def key_kernel(kh_ref, vh_ref, wk_ref, ds1_ref, after_ref, gk_ref):
@@ -293,12 +296,13 @@
     barrier = greet(count, me, axes)
     lane = lax.broadcasted_iota(jnp.int32, (1, width), 1)
     packed = jnp.zeros(mine.shape[1:], F32)
+    shape = mine.shape
     for h in range(heads):
         own = sum(part[n, h] for part in parts for n in range(part.shape[0]))
-        mine[h] = own[:, :width]
+        mine[h] = own[:, :width].astype(BF16)
         norm = -jnp.sum(own[:, width:], 1, keepdims=True) if later else own[:, width:]
         packed = jnp.where(lane == h, norm, packed)
-    mine[heads] = packed
+    mine[heads], mine[heads + 1] = halves(packed)
     pl.semaphore_wait(barrier, count - 1)
 
     def copy(sender, target):
@@ -311,7 +315,6 @@
             device_id_type=pl.DeviceIdType.MESH,
         )
 
-    slots[me] = jnp.zeros(mine.shape, F32)
     if later:
         first_to, end_to, first_from, end_from = 0, me, me + 1, count
     else:
@@ -327,20 +330,20 @@
 
     def received(p, total):
         copy(p, lax.rem(me + 1, count)).wait_recv()
-        return total + slots[p]
+        return total + slots[p].astype(F32)
 
     lax.fori_loop(first_to, end_to, send, 0)
-    total = lax.fori_loop(first_from, end_from, received, jnp.zeros(mine.shape, F32))
+    total = lax.fori_loop(first_from, end_from, received, jnp.zeros(shape, F32))
     lax.fori_loop(first_to, end_to, sent, 0)
     for h in range(heads):
-        norm = jnp.sum(jnp.where(lane == h, total[heads], 0.0), 1, keepdims=True)
+        norm = jnp.sum(jnp.where(lane == h, total[heads] + total[heads + 1], 0.0), 1, keepdims=True)
         out_ref[h] = jnp.concatenate([total[h], jnp.broadcast_to(norm, total[h].shape)], 1)
 
 
 def sum_of_others(parts, axis, later, collective_id):
     heads, rank, twice = parts[0].shape[1:]
     count = lax.axis_size(axis)
-    block = (heads + 1, rank, twice // 2)
+    block = (heads + 2, rank, twice // 2)
     vmem = pl.BlockSpec(memory_space=pltpu.VMEM)
     return pl.pallas_call(
         functools.partial(others_kernel, axis, later),
@@ -349,8 +352,8 @@
         out_specs=vmem,
         out_shape=jax.ShapeDtypeStruct((heads, rank, twice), F32),
         scratch_shapes=[
-            pltpu.VMEM(block, F32),
-            pltpu.VMEM((count,) + block, F32),
+            pltpu.VMEM(block, BF16),
+            pltpu.VMEM((count,) + block, BF16),
             pltpu.SemaphoreType.DMA((count,)),
             pltpu.SemaphoreType.DMA((count,)),
         ],
@@ -361,7 +364,7 @@
     )(*parts)
 
 
-def reduce_kernel(axes, gq0, gq1, gk0, gk1, gk2, out_ref, mine, slots, done, out_sem, in_sem, back_sem, res_sem):
+def reduce_kernel(axes, gq0, gq1, gk0, gk1, gk2, gq_ref, gk_ref, mine, slots, done, out_sem, in_sem, back_sem, res_sem):
     heads = gq0.shape[0]
     chunks = 2 * heads
     me, count = flat_id(axes)
@@ -434,7 +437,8 @@
 
         lax.fori_loop(1, count, sent, 0)
 
-    out_ref[...] = done[...]
+    gq_ref[...] = done[:heads]
+    gk_ref[...] = done[heads:]
 
 
 def sum_over_all(grads, axes):
@@ -448,8 +452,8 @@
         functools.partial(reduce_kernel, axes),
         name="sum_grads",
         in_specs=[vmem] * len(grads),
-        out_specs=vmem,
-        out_shape=jax.ShapeDtypeStruct(whole, F32),
+        out_specs=[vmem, vmem],
+        out_shape=[jax.ShapeDtypeStruct((heads, rank, width), F32)] * 2,
         scratch_shapes=[
             pltpu.VMEM(whole, F32),
             pltpu.VMEM((count, per, rank, width), F32),
@@ -495,20 +499,17 @@
     me = lax.axis_index("seq")
     where = jnp.stack([me, jnp.int32(tiles)]).astype(jnp.int32)
     ring = [(a, a + 1) for a in range(peers - 1)]
-    kp, vp = lax.ppermute((k_rows[tokens - TILE :], v_rows[tokens - TILE :]), "seq", ring)
+    halo = lax.ppermute(jnp.stack([k_rows[tokens - TILE :], v_rows[tokens - TILE :]]), "seq", ring)
     wq = jnp.swapaxes(query_map, 1, 2)
     wk = jnp.swapaxes(key_map, 1, 2)
     kh, vh, total = local_states(k_rows, v_rows, wk)
     states = sum_of_others([total[None]], "seq", False, 0)
-    rest = attend(1, tiles - 1, False, counts, where, q_rows, kh, vh, kh, vh, cot, wq, wk, states)
-    head = attend(0, 1, True, counts, where, q_rows, kh, vh, kp, vp, cot, wq, wk, states)
+    rest = attend(1, tiles - 1, None, counts, where, q_rows, kh, vh, kh, vh, cot, wq, wk, states)
+    head = attend(0, 1, rest[0], counts, where, q_rows, kh, vh, halo, halo, cot, wq, wk, states)
     after = sum_of_others([head[1], rest[1]], "seq", True, 1)
     gk = key_grads(kh, vh, wk, rest[1], after)
-    heads, rank, width = wq.shape
     grads = sum_over_all([head[2], rest[2], head[3], rest[3], gk], ("seq", "batch"))
-    grads = jnp.swapaxes(grads.reshape(2, heads, rank, width), 2, 3)
-    out = jnp.concatenate([head[0], rest[0]], 0)
-    return out[None], grads[0], grads[1]
+    return head[0][None], jnp.swapaxes(grads[0], 1, 2), jnp.swapaxes(grads[1], 1, 2)
 
 
 def solution(mesh):

time: 115 us -> 98.6 us (0.86)
  Pallas kernels: 98.1 us -> 86.7 us
  starting transfers between devices: 8.36 us -> 4.97 us
  other arithmetic: 2.06 us -> 0.65 us
    pallas_call x2, Pallas kernels: 26.8 us -> 22.4 us  [attend(): pl.pallas_call(functools.partial(main_kernel, first, halo), name='attend_...]
    pallas_call x2, Pallas kernels: 39.2 us -> 35.4 us  [sum_of_others(): pl.pallas_call(functools.partial(others_kernel, axis, later), name='later...]
    ppermute x2 -> x1, starting transfers between devices: 8.36 us -> 4.97 us  [body(): lax.ppermute(jnp.stack([k_rows[tokens - TILE:], v_rows[tokens - TILE:]]),...]
    pallas_call x1, Pallas kernels: 20.5 us -> 17.5 us  [sum_over_all(): pl.pallas_call(functools.partial(reduce_kernel, axes), name='sum_grads',...]
    unnamed x8 -> x4, local copies, waits for them, and re-layouts: 1.6 us -> 3.9 us
    squeeze x1 -> x0, local copies, waits for them, and re-layouts: 1.53 us -> none  [body(): return (out[None], grads[0], grads[1])]
    broadcast_in_dim x1 -> x0, other arithmetic: 1.5 us -> none  [body(): return (out[None], grads[0], grads[1])]
  transfers between devices with their start and end apart: 2 -> 1, of which waited for: 0 -> 0; matrix products, arithmetic and copies ran while one was open for 1% -> 1% of each run, Pallas kernels for 34% -> 40%
where the time goes in v3:
time: 98.6 us; the launch traced here: 98.1 us
  Pallas kernels  86.7 us (88%)
  local copies, waits for them, and re-layouts  5.09 us (5%)
  starting transfers between devices  4.97 us (5%)
    pallas_call x2, Pallas kernels, sum_of_others(): pl.pallas_call(functools.partial(others_kernel, axis, later), name='later...  35.4 us
    pallas_call x2, Pallas kernels, attend(): pl.pallas_call(functools.partial(main_kernel, first, halo), name='attend_...  22.4 us
    pallas_call x1, Pallas kernels, sum_over_all(): pl.pallas_call(functools.partial(reduce_kernel, axes), name='sum_grads',...  17.5 us
    pallas_call x1, Pallas kernels, local_states(): pl.pallas_call(state_kernel, name='local_states', grid=(tokens // TILE,),...  6.32 us
    pallas_call x1, Pallas kernels, key_grads(): pl.pallas_call(key_kernel, name='key_grads', grid=(heads // group,), in_s...  5.12 us
    ppermute x1, starting transfers between devices, body(): lax.ppermute(jnp.stack([k_rows[tokens - TILE:], v_rows[tokens - TILE:]]),...  4.97 us
    unnamed x4, local copies, waits for them, and re-layouts  3.9 us
  transfers between devices with their start and end apart: 1, of which 0 were waited for; matrix products, arithmetic and copies ran while one was open for 1% of the time, Pallas kernels for 40%

profile of v3, /device:TPU:0, one launch (start us, length us, event | category | flops | bytes accessed | tf_op | source)
XLA Modules:
  0.0 98.1 jit_solution(555866390427515050)
XLA Ops:
  0.6 0.0 slice-start
  0.6 0.0 slice-start.1
  0.7 1.0 %slice-done = bf16[1,128,16,128]{3,2,1,0:T(8,128)(2,1)S(1)} async-done(((bf16[1,512,16,128]{3,2,1,0:T(8,128)(2,1)}), bf16[1,128,16,128]{3,2,1,0:T(8,128)(2,1)S(1)}, s32[]{:S(2)}) %slice-start) | async-done | bytes 524312 | tf_op jit(solution)/shard_map/slice | solution.py:502
  1.7 0.2 slice-done.1
  1.8 0.1 pad_maximum_fusion
  1.9 5.0 %collective-permute-start = (bf16[2,128,16,128]{3,2,1,0:T(8,128)(2,1)S(1)}, bf16[2,128,16,128]{3,2,1,0:T(8,128)(2,1)S(1)}, u32[]{:S(2)}, u32[]{:S(2)}) collective-permute-start(bf16[2,128,16,128]{3,2,1,0:T(8,128)(2,1)S(1)} %pad_maximum_fusion), channel_id=1, source_target_pairs={{0,4},{4,8},{8,12},{12,16},{16,20},{20,24},{24,28},{1,5},{5,9},{9,... | collective-permute-start | bytes 3145736 | tf_op jit(solution)/shard_map/ppermute | solution.py:502
  6.9 6.3 %local_states.1 = (bf16[16,512,128]{2,1,0:T(8,128)(2,1)}, bf16[16,512,128]{2,1,0:T(8,128)(2,1)}, f32[16,8,256]{2,1,0:T(8,128)}) custom-call(bf16[512,16,128]{2,1,0:T(8,128)(2,1)} %bitcast.16, bf16[512,16,128]{2,1,0:T(8,128)(2,1)} %bitcast.17, bf16[16,8,128]{2,1,0:T(8,128)(2,1)} %bitcast.19), custom_call_target="tpu_custom_call" | custom-call | flops 1000000000 | bytes 8388608 | tf_op jit(solution)/shard_map/local_states/pallas_call | solution.py:85
  13.2 17.7 %earlier_states.1.states_ref = f32[16,8,256]{2,1,0:T(8,128)} custom-call(f32[1,16,8,256]{3,2,1,0:T(8,128)} %bitcast.25), custom_call_target="tpu_custom_call" | custom-call | flops 10000000 | bytes 1048576 | tf_op jit(solution)/shard_map/earlier_states/pallas_call | solution.py:348
  30.9 0.6 pad_add_fusion.where_ref
  31.5 15.2 %attend_rest.1 = (bf16[512,16,128]{2,1,0:T(8,128)(2,1)}, f32[3,16,8,256]{3,2,1,0:T(8,128)}, f32[16,8,128]{2,1,0:T(8,128)}, f32[16,8,128]{2,1,0:T(8,128)}) custom-call(s32[16,32]{1,0:T(8,128)} %bitcast.28, s32[2]{0:T(128)} %pad_add_fusion.where_ref, bf16[512,16,128]{2,1,0:T(8,128)(2,1)} %bitcast.12, ...), custom_call_target="tpu_custom_call" | custom-call | flops 3000000000 | bytes 12582912 | tf_op jit(solution)/shard_map/attend_rest/pallas_call | solution.py:213
  46.7 0.0 collective-permute-done.kp_ref.vp_ref
  46.8 0.0 copy-start
  46.8 1.0 copy-done
  47.7 7.1 %attend_first.1 = (bf16[512,16,128]{2,1,0:T(8,128)(2,1)}, f32[1,16,8,256]{3,2,1,0:T(8,128)}, f32[16,8,128]{2,1,0:T(8,128)}, f32[16,8,128]{2,1,0:T(8,128)}) custom-call(s32[16,32]{1,0:T(8,128)} %bitcast.29, s32[2]{0:T(128)} %pad_add_fusion.where_ref, bf16[512,16,128]{2,1,0:T(8,128)(2,1)} %bitcast.13, ...), custom_call_target="tpu_custom_call", output_to_operand_aliasing={{0}: (11, {})} | custom-call | flops 1000000000 | bytes 4194304 | tf_op jit(solution)/shard_map/attend_first/pallas_call | solution.py:213
  54.9 17.7 %later_grads.1.after_ref = f32[16,8,256]{2,1,0:T(8,128)} custom-call(f32[1,16,8,256]{3,2,1,0:T(8,128)} %get-tuple-element.26.refs_0_, f32[3,16,8,256]{3,2,1,0:T(8,128)} %get-tuple-element.25.refs_1_.ds1_ref), custom_call_target="tpu_custom_call" | custom-call | flops 10000000 | bytes 1048576 | tf_op jit(solution)/shard_map/later_grads/pallas_call | solution.py:348
  72.5 5.1 %key_grads.1.gk2 = f32[16,8,128]{2,1,0:T(8,128)} custom-call(bf16[16,512,128]{2,1,0:T(8,128)(2,1)} %get-tuple-element.16.k_ref.kp_ref.kh_ref, bf16[16,512,128]{2,1,0:T(8,128)(2,1)} %get-tuple-element.17.v_ref.vp_ref.vh_ref, bf16[16,8,128]{2,1,0:T(8,128)(2,1)} %bitcast.22, f32[3,16,8,256]{3,2,1,0:T(8,128)} %get-tuple-element.25.refs_1_.ds1_ref, ...), custom_call_target="tpu_custom_call" | custom-call | flops 1000000000 | bytes 8388608 | tf_op jit(solution)/shard_map/key_grads/pallas_call | solution.py:479
  77.6 17.5 %sum_grads.1 = (f32[16,8,128]{2,1,0:T(8,128)}, f32[16,8,128]{2,1,0:T(8,128)}) custom-call(f32[16,8,128]{2,1,0:T(8,128)} %get-tuple-element.21.gq0, f32[16,8,128]{2,1,0:T(8,128)} %get-tuple-element.22.gq1, f32[16,8,128]{2,1,0:T(8,128)} %get-tuple-element.23.gk0, f32[16,8,128]{2,1,0:T(8,128)} %get-tuple-element.24.gk1, f32[16,8,128]{2,1,0:T(8,128)} %key_grads.1.gk2), custom_call_target="tpu_custom_call" | custom-call | flops 10000000 | bytes 1048576 | tf_op jit(solution)/shard_map/sum_grads/pallas_call | solution.py:451
  95.2 1.5 %copy.14 = f32[16,128,8]{1,2,0:T(8,128)} copy(f32[16,128,8]{1,2,0:T(8,128)} %bitcast.27) | data formatting | bytes 131072
  96.6 1.5 %copy.15 = f32[16,128,8]{1,2,0:T(8,128)} copy(f32[16,128,8]{1,2,0:T(8,128)} %bitcast.26) | data formatting | bytes 131072
Async XLA Ops:
  0.6 1.0 %slice-start = ((bf16[1,512,16,128]{3,2,1,0:T(8,128)(2,1)}), bf16[1,128,16,128]{3,2,1,0:T(8,128)(2,1)S(1)}, s32[]{:S(2)}) async-start(bf16[1,512,16,128]{3,2,1,0:T(8,128)(2,1)} %param.8), calls=%async_computation | async-start | bytes 1048576 | tf_op jit(solution)/shard_map/slice | solution.py:502
  0.6 1.2 %slice-start.1 = ((bf16[1,512,16,128]{3,2,1,0:T(8,128)(2,1)}), bf16[1,128,16,128]{3,2,1,0:T(8,128)(2,1)S(1)}, s32[]{:S(2)}) async-start(bf16[1,512,16,128]{3,2,1,0:T(8,128)(2,1)} %param.9), calls=%async_computation.1 | async-start | bytes 1048576 | tf_op jit(solution)/shard_map/slice | solution.py:502
  1.9 44.8 %collective-permute-start = (bf16[2,128,16,128]{3,2,1,0:T(8,128)(2,1)S(1)}, bf16[2,128,16,128]{3,2,1,0:T(8,128)(2,1)S(1)}, u32[]{:S(2)}, u32[]{:S(2)}) collective-permute-start(bf16[2,128,16,128]{3,2,1,0:T(8,128)(2,1)S(1)} %pad_maximum_fusion), channel_id=1, source_target_pairs={{0,4},{4,8},{8,12},{12,16},{16,20},{20,24},{24,28},{1,5},{5,9},{9,... | collective-permute-start | bytes 3145736 | tf_op jit(solution)/shard_map/ppermute | solution.py:502
  46.8 1.0 copy-start
